TPU v7x, 16 devices: a 4x2x1 block of a 4x4x8 slice. The times are simulated.
16 devices in a mesh: dp: 2 (over y, z), seq: 8 (over x, core).
Axes of the slice: x: 4, y: 2, z: 1, core: 2. Of those that a mesh axis runs over, the one named last changes fastest.
The devices are a block of a 4x4x8 slice.
Arguments:
- enc_out: bfloat16 [128, 64, 512], P('dp', 'seq'), parts along dimension 0
- pred_out: bfloat16 [128, 8, 640], P('dp'), parts along dimension 0
- w_enc: bfloat16 [512, 640], replicated
- w_pred: bfloat16 [640, 640], replicated
- w_out: bfloat16 [640, 1024], replicated
- labels: int32 [128, 7], P('dp'), parts along dimension 0
- frame_len: int32 [128], P('dp'), parts along dimension 0
- label_len: int32 [128], P('dp'), parts along dimension 0
Outputs:
- output 1: float32 [128], P('dp'), parts along dimension 0
- output 2: bfloat16 [128, 64, 512], P('dp', 'seq'), parts along dimension 0
- output 3: float32 [1024, 640], P('dp'), parts along dimension 0
- output 4: float32 [1280, 640], P('dp'), parts along dimension 0
- output 5: float32 [1280, 1024], P('dp'), parts along dimension 0
There are 2 independent parts. A program takes and returns all parts, laid end to end along the dimension named above; an argument that names none is the same for every part.
All inputs are finite; a program needn't handle non-finite values.
Results may differ from a plain program's by a relative error of at most 0.0139293.
Values are sent between devices in bfloat16 or wider.
A program may use at most 768 MiB of HBM per device.

v0:
```python
import jax
import jax.numpy as jnp
from jax import lax
from jax.sharding import PartitionSpec as P

NEG_FILL = -1.0e30


def label_prefix(lab_lp):
    zero_col = jnp.zeros_like(lab_lp[:, :1])
    return jnp.concatenate([zero_col, jnp.cumsum(lab_lp[:, :-1], axis=1)], axis=1)


def label_weights(labels, w_out):
    n_utt = labels.shape[0]
    lab_ids = jnp.concatenate([labels, jnp.full((n_utt, 1), -1, jnp.int32)], axis=1)
    onehot = (lab_ids[:, :, None] == lax.broadcasted_iota(jnp.int32, (1, 1, w_out.shape[1]), 2)).astype(jnp.bfloat16)
    lab_w = jnp.einsum('buv,jv->buj', onehot, w_out, preferred_element_type=jnp.float32).astype(jnp.bfloat16)
    return lab_ids, lab_w


def joint_lattice(enc_blk, act_g, lab_w, w_enc, w_out):
    act_f = jnp.einsum('bth,hj->btj', enc_blk, w_enc, preferred_element_type=jnp.float32).astype(jnp.bfloat16)
    hidden = jnp.tanh(act_f[:, :, None, :].astype(jnp.float32) + act_g[:, None, :, :].astype(jnp.float32)).astype(jnp.bfloat16)
    logits = jnp.einsum('btuj,jv->btuv', hidden, w_out, preferred_element_type=jnp.float32)
    log_norm = jax.nn.logsumexp(logits, axis=-1)
    soft_probs = jnp.exp(logits - log_norm[..., None])
    blank_lp = logits[..., 0] - log_norm
    lab_lp = jnp.einsum('btuj,buj->btu', hidden, lab_w, preferred_element_type=jnp.float32) - log_norm
    return hidden, soft_probs, blank_lp, lab_lp


def alpha_rows(x_in, blank_lp, lab_lp):
    def frame_step(x_prev, frame_in):
        frame_blank, frame_lab = frame_in
        lab_sum = label_prefix(frame_lab)
        alpha_t = lab_sum + lax.cumlogsumexp(x_prev - lab_sum, axis=1)
        return alpha_t + frame_blank, alpha_t
    x_out, alphas = lax.scan(frame_step, x_in, (jnp.swapaxes(blank_lp, 0, 1), jnp.swapaxes(lab_lp, 0, 1)))
    return x_out, jnp.swapaxes(alphas, 0, 1)


def beta_rows(next_in, blank_lp, lab_lp, frame_ids, frame_len, boundary):
    def frame_step(next_row, frame_in):
        frame_blank, frame_lab, frame_id = frame_in
        lab_sum = label_prefix(frame_lab)
        beta_row = lax.cumlogsumexp(next_row + frame_blank + lab_sum, axis=1, reverse=True) - lab_sum
        beta_row = jnp.where((frame_id >= frame_len)[:, None], boundary, beta_row)
        return beta_row, (beta_row, next_row)
    first_row, (betas, beta_next) = lax.scan(frame_step, next_in, (jnp.swapaxes(blank_lp, 0, 1), jnp.swapaxes(lab_lp, 0, 1), frame_ids), reverse=True)
    return first_row, jnp.swapaxes(betas, 0, 1), jnp.swapaxes(beta_next, 0, 1)


def occupancy(alphas, betas, beta_next, blank_lp, lab_lp, log_prob, frame_ok):
    beta_up = jnp.concatenate([betas[:, :, 1:], jnp.full_like(betas[:, :, :1], NEG_FILL)], axis=2)
    norm_shift = log_prob[:, None, None]
    occ_blank = jnp.where(frame_ok, jnp.exp(jnp.minimum(alphas + blank_lp + beta_next - norm_shift, 0.0)), 0.0)
    occ_lab = jnp.where(frame_ok, jnp.exp(jnp.minimum(alphas + lab_lp + beta_up - norm_shift, 0.0)), 0.0)
    return occ_blank, occ_lab


def joint_backward(enc_blk, hidden, soft_probs, occ_blank, occ_lab, lab_ids, w_enc, w_out):
    vocab_ids = lax.broadcasted_iota(jnp.int32, (1, 1, 1, soft_probs.shape[-1]), 3)
    d_logits = (soft_probs * (occ_blank + occ_lab)[..., None] - jnp.where(vocab_ids == 0, occ_blank[..., None], 0.0) - jnp.where(vocab_ids == lab_ids[:, None, :, None], occ_lab[..., None], 0.0)).astype(jnp.bfloat16)
    d_hidden = jnp.einsum('btuv,jv->btuj', d_logits, w_out, preferred_element_type=jnp.float32)
    d_pre = (d_hidden * (1.0 - jnp.square(hidden.astype(jnp.float32)))).astype(jnp.bfloat16)
    d_act_f = jnp.sum(d_pre, axis=2, dtype=jnp.float32).astype(jnp.bfloat16)
    d_act_g = jnp.sum(d_pre, axis=1, dtype=jnp.float32)
    grad_enc = jnp.einsum('btj,hj->bth', d_act_f, w_enc, preferred_element_type=jnp.float32).astype(jnp.bfloat16)
    gw_enc = jnp.einsum('bth,btj->hj', enc_blk, d_act_f, preferred_element_type=jnp.float32)
    gw_out = jnp.einsum('btuj,btuv->jv', hidden, d_logits, preferred_element_type=jnp.float32)
    return grad_enc, gw_enc, gw_out, d_act_g


def solution(mesh):
    seq_size = mesh.shape['seq']
    fwd_pairs = [(src, src + 1) for src in range(seq_size - 1)]
    bwd_pairs = [(src + 1, src) for src in range(seq_size - 1)]

    def local_fn(enc_out, pred_out, w_enc, w_pred, w_out, labels, frame_len, label_len):
        seq_idx = lax.axis_index('seq')
        n_utt, n_loc, _ = enc_out.shape
        lab_pos = pred_out.shape[1]
        lab_ids, lab_w = label_weights(labels, w_out)
        act_g = jnp.einsum('buh,hj->buj', pred_out, w_pred, preferred_element_type=jnp.float32).astype(jnp.bfloat16)
        hidden, soft_probs, blank_lp, lab_lp = joint_lattice(enc_out, act_g, lab_w, w_enc, w_out)
        pos_ids = lax.broadcasted_iota(jnp.int32, (n_utt, lab_pos), 1)
        neg_rows = jnp.full((n_utt, lab_pos), NEG_FILL, jnp.float32)
        init_x = jnp.where(pos_ids == 0, 0.0, neg_rows)
        boundary = jnp.where(pos_ids == label_len[:, None], 0.0, neg_rows)
        frame_ids = seq_idx * n_loc + jnp.arange(n_loc, dtype=jnp.int32)

        def alpha_hop(hop_idx, x_in):
            x_out, _ = alpha_rows(x_in, blank_lp, lab_lp)
            received = lax.ppermute(x_out, 'seq', fwd_pairs)
            return jnp.where(seq_idx == 0, init_x, received)

        x_in = lax.fori_loop(0, seq_size - 1, alpha_hop, init_x)
        _, alphas = alpha_rows(x_in, blank_lp, lab_lp)

        def beta_hop(hop_idx, next_in):
            first_row, _, _ = beta_rows(next_in, blank_lp, lab_lp, frame_ids, frame_len, boundary)
            received = lax.ppermute(first_row, 'seq', bwd_pairs)
            return jnp.where(seq_idx == seq_size - 1, boundary, received)

        next_in = lax.fori_loop(0, seq_size - 1, beta_hop, boundary)
        first_row, betas, beta_next = beta_rows(next_in, blank_lp, lab_lp, frame_ids, frame_len, boundary)
        log_prob = lax.psum(jnp.where(seq_idx == 0, first_row[:, 0], 0.0), 'seq')
        frame_ok = (frame_ids[None, :] < frame_len[:, None])[:, :, None]
        occ_blank, occ_lab = occupancy(alphas, betas, beta_next, blank_lp, lab_lp, log_prob, frame_ok)
        grad_enc, gw_enc, gw_out, d_act_g = joint_backward(enc_out, hidden, soft_probs, occ_blank, occ_lab, lab_ids, w_enc, w_out)
        gw_pred = jnp.einsum('buh,buj->hj', pred_out, d_act_g, preferred_element_type=jnp.float32)
        gw_enc, gw_pred, gw_out = lax.psum((gw_enc, gw_pred, gw_out), 'seq')
        return -log_prob, grad_enc, gw_enc, gw_pred, gw_out

    in_specs = (P('dp', 'seq', None), P('dp', None, None), P(None, None), P(None, None), P(None, None), P('dp', None), P('dp'), P('dp'))
    out_specs = (P('dp'), P('dp', 'seq', None), P('dp', None), P('dp', None), P('dp', None))
    return jax.shard_map(local_fn, mesh=mesh, in_specs=in_specs, out_specs=out_specs, check_vma=False)
```

profile of v0, /device:TPU:113, one launch (start us, length us, event | category | flops | bytes accessed | tf_op | source)
XLA Modules:
  0.0 387.1 jit_solution(12287310377476493688)
XLA Ops:
  14.2 10.5 %fusion.47 = (f32[64,8,8]{2,1,0:T(8,128)S(1)}, f32[64,8,8,1024]{3,2,1,0:T(8,128)}) fusion(bf16[640,1024]{1,0:T(8,128)(2,1)S(1)} %copy-done, f32[64,8,640]{2,1,0:T(8,128)S(1)} %fusion.15, f32[64,8,640]{2,1,0:T(8,128)S(1)} %fusion.16), kind=kOutput, calls=%fused_computation.88 | convolution fusion | flops 5378142208 | bytes 20725760 | tf_op jit(solution)/shard_map/btuj,jv->btuv/dot_general | solution.py:25
  31.6 7.4 %exponential_reduce_fusion = f32[64,8,8]{2,1,0:T(8,128)S(1)} fusion(f32[64,8,8,1024]{3,2,1,0:T(8,128)} %get-tuple-element.856, f32[64,8,8]{2,1,0:T(8,128)S(1)} %is-finite_select_fusion.1), kind=kLoop, calls=%fused_computation.31 | loop fusion | flops 8384512 | bytes 16809984 | tf_op jit(solution)/shard_map/reduce_sum | solution.py:26
  42.9 3.7 copy.81
  50.8 122.7 %while.105 = (s32[]{:T(128)}, f32[64,8]{0,1:T(8,128)S(1)}, pred[]{:T(512)}, f32[64,8,8]{0,2,1:T(8,128)S(1)}, f32[64,8,8]{0,2,1:T(8,128)S(1)}, /*index=5*/s32[64]...) while((s32[]{:T(128)}, f32[64,8]{0,1:T(8,128)S(1)}, ...), condition=%wide.region_7.8_spmd.clone, body=%wide.region_2.7_spmd.clone.sunk | while | flops 36045 | bytes 43355 | solution.py:106
  50.9 12.4 %while.109 = (s32[]{:T(128)}, f32[64,8]{0,1:T(8,128)S(1)}, s32[8]{0:T(128)S(1)}, s32[64]{0:T(128)S(1)}, f32[8,64,8]{1,2,0:T(8,128)S(1)}, /*index=5*/f32[8,64,8]{...) while((s32[]{:T(128)}, f32[64,8]{0,1:T(8,128)S(1)}, ...), condition=%wide.region_6.6_spmd, body=%wide.region_3.5_spmd.sunk | while | flops 33475 | bytes 28193 | solution.py:50
  69.2 12.4 %while.109 = (s32[]{:T(128)}, f32[64,8]{0,1:T(8,128)S(1)}, s32[8]{0:T(128)S(1)}, s32[64]{0:T(128)S(1)}, f32[8,64,8]{1,2,0:T(8,128)S(1)}, /*index=5*/f32[8,64,8]{...) while((s32[]{:T(128)}, f32[64,8]{0,1:T(8,128)S(1)}, ...), condition=%wide.region_6.6_spmd, body=%wide.region_3.5_spmd.sunk | while | flops 33475 | bytes 28193 | solution.py:50
  86.6 12.4 %while.109 = (s32[]{:T(128)}, f32[64,8]{0,1:T(8,128)S(1)}, s32[8]{0:T(128)S(1)}, s32[64]{0:T(128)S(1)}, f32[8,64,8]{1,2,0:T(8,128)S(1)}, /*index=5*/f32[8,64,8]{...) while((s32[]{:T(128)}, f32[64,8]{0,1:T(8,128)S(1)}, ...), condition=%wide.region_6.6_spmd, body=%wide.region_3.5_spmd.sunk | while | flops 33475 | bytes 28193 | solution.py:50
  104.0 12.4 %while.109 = (s32[]{:T(128)}, f32[64,8]{0,1:T(8,128)S(1)}, s32[8]{0:T(128)S(1)}, s32[64]{0:T(128)S(1)}, f32[8,64,8]{1,2,0:T(8,128)S(1)}, /*index=5*/f32[8,64,8]{...) while((s32[]{:T(128)}, f32[64,8]{0,1:T(8,128)S(1)}, ...), condition=%wide.region_6.6_spmd, body=%wide.region_3.5_spmd.sunk | while | flops 33475 | bytes 28193 | solution.py:50
  121.4 12.4 %while.109 = (s32[]{:T(128)}, f32[64,8]{0,1:T(8,128)S(1)}, s32[8]{0:T(128)S(1)}, s32[64]{0:T(128)S(1)}, f32[8,64,8]{1,2,0:T(8,128)S(1)}, /*index=5*/f32[8,64,8]{...) while((s32[]{:T(128)}, f32[64,8]{0,1:T(8,128)S(1)}, ...), condition=%wide.region_6.6_spmd, body=%wide.region_3.5_spmd.sunk | while | flops 33475 | bytes 28193 | solution.py:50
  138.8 12.4 %while.109 = (s32[]{:T(128)}, f32[64,8]{0,1:T(8,128)S(1)}, s32[8]{0:T(128)S(1)}, s32[64]{0:T(128)S(1)}, f32[8,64,8]{1,2,0:T(8,128)S(1)}, /*index=5*/f32[8,64,8]{...) while((s32[]{:T(128)}, f32[64,8]{0,1:T(8,128)S(1)}, ...), condition=%wide.region_6.6_spmd, body=%wide.region_3.5_spmd.sunk | while | flops 33475 | bytes 28193 | solution.py:50
  156.2 12.4 %while.109 = (s32[]{:T(128)}, f32[64,8]{0,1:T(8,128)S(1)}, s32[8]{0:T(128)S(1)}, s32[64]{0:T(128)S(1)}, f32[8,64,8]{1,2,0:T(8,128)S(1)}, /*index=5*/f32[8,64,8]{...) while((s32[]{:T(128)}, f32[64,8]{0,1:T(8,128)S(1)}, ...), condition=%wide.region_6.6_spmd, body=%wide.region_3.5_spmd.sunk | while | flops 33475 | bytes 28193 | solution.py:50
  173.6 13.2 %while.106 = (s32[]{:T(128)}, f32[64,8]{0,1:T(8,128)S(1)}, f32[8,64,8]{1,2,0:T(8,128)S(1)}, f32[8,64,8]{1,2,0:T(8,128)S(1)}, s32[8]{0:T(128)S(1)}, /*index=5*/s3...) while((s32[]{:T(128)}, f32[64,8]{0,1:T(8,128)S(1)}, ...), condition=%wide.region_11.12_spmd.clone, body=%wide.region_8.11_spmd.clone.sunk | while | flops 34499 | bytes 45813 | solution.py:50
  186.8 11.7 %psum.28 = f32[64]{0:T(128)} all-reduce(f32[64]{0:T(128)S(1)} %fusion.42), channel_id=1, replica_groups=mesh['dp'=2,'seq'=8] {'seq'}, use_global_device_ids=true, to_apply=%region_12.13 | all-reduce | flops 64 | bytes 512 | tf_op jit(solution)/shard_map/psum | solution.py:108
  200.1 52.5 %while.108 = (s32[]{:T(128)}, f32[64,8]{0,1:T(8,128)S(1)}, pred[]{:T(512)}, f32[64,8,8]{0,2,1:T(8,128)S(1)}, f32[64,8,8]{0,2,1:T(8,128)S(1)}, /*index=5*/f32[8]{...) while((s32[]{:T(128)}, f32[64,8]{0,1:T(8,128)S(1)}, pred[]{:T(512)}, ...), condition=%wide.region_18.19_spmd.clone, body=%wide.region_13.18_spmd.clone.sunk | while | flops 33412 | bytes 38235 | solution.py:98
  208.7 3.9 %collective-permute-start = (f32[64,8]{0,1:T(8,128)S(1)}, f32[64,8]{0,1:T(8,128)S(1)}, u32[]{:S(2)}, u32[]{:S(2)}) collective-permute-start(f32[64,8]{0,1:T(8,128)S(1)} %get-tuple-element.1120), channel_id=1, source_target_pairs={{0,1},{1,2},{2,3},{3,4},{4,5},{5,6},{6,7},{8,9},{9,10},{10,11},{11... | collective-permute-start | bytes 6152 | tf_op jit(solution)/shard_map/while/body/eval_jaxpr/ppermute | solution.py:95
  216.1 4.2 %collective-permute-start = (f32[64,8]{0,1:T(8,128)S(1)}, f32[64,8]{0,1:T(8,128)S(1)}, u32[]{:S(2)}, u32[]{:S(2)}) collective-permute-start(f32[64,8]{0,1:T(8,128)S(1)} %get-tuple-element.1120), channel_id=1, source_target_pairs={{0,1},{1,2},{2,3},{3,4},{4,5},{5,6},{6,7},{8,9},{9,10},{10,11},{11... | collective-permute-start | bytes 6152 | tf_op jit(solution)/shard_map/while/body/eval_jaxpr/ppermute | solution.py:95
  223.8 4.2 %collective-permute-start = (f32[64,8]{0,1:T(8,128)S(1)}, f32[64,8]{0,1:T(8,128)S(1)}, u32[]{:S(2)}, u32[]{:S(2)}) collective-permute-start(f32[64,8]{0,1:T(8,128)S(1)} %get-tuple-element.1120), channel_id=1, source_target_pairs={{0,1},{1,2},{2,3},{3,4},{4,5},{5,6},{6,7},{8,9},{9,10},{10,11},{11... | collective-permute-start | bytes 6152 | tf_op jit(solution)/shard_map/while/body/eval_jaxpr/ppermute | solution.py:95
  231.5 4.2 %collective-permute-start = (f32[64,8]{0,1:T(8,128)S(1)}, f32[64,8]{0,1:T(8,128)S(1)}, u32[]{:S(2)}, u32[]{:S(2)}) collective-permute-start(f32[64,8]{0,1:T(8,128)S(1)} %get-tuple-element.1120), channel_id=1, source_target_pairs={{0,1},{1,2},{2,3},{3,4},{4,5},{5,6},{6,7},{8,9},{9,10},{10,11},{11... | collective-permute-start | bytes 6152 | tf_op jit(solution)/shard_map/while/body/eval_jaxpr/ppermute | solution.py:95
  239.2 4.2 %collective-permute-start = (f32[64,8]{0,1:T(8,128)S(1)}, f32[64,8]{0,1:T(8,128)S(1)}, u32[]{:S(2)}, u32[]{:S(2)}) collective-permute-start(f32[64,8]{0,1:T(8,128)S(1)} %get-tuple-element.1120), channel_id=1, source_target_pairs={{0,1},{1,2},{2,3},{3,4},{4,5},{5,6},{6,7},{8,9},{9,10},{10,11},{11... | collective-permute-start | bytes 6152 | tf_op jit(solution)/shard_map/while/body/eval_jaxpr/ppermute | solution.py:95
  246.9 4.2 %collective-permute-start = (f32[64,8]{0,1:T(8,128)S(1)}, f32[64,8]{0,1:T(8,128)S(1)}, u32[]{:S(2)}, u32[]{:S(2)}) collective-permute-start(f32[64,8]{0,1:T(8,128)S(1)} %get-tuple-element.1120), channel_id=1, source_target_pairs={{0,1},{1,2},{2,3},{3,4},{4,5},{5,6},{6,7},{8,9},{9,10},{10,11},{11... | collective-permute-start | bytes 6152 | tf_op jit(solution)/shard_map/while/body/eval_jaxpr/ppermute | solution.py:95
  261.2 18.2 %fusion.48 = (bf16[64,8,640]{2,1,0:T(8,128)(2,1)}, bf16[64,8,8,640]{3,2,1,0:T(8,128)(2,1)}) fusion(f32[64,8,640]{2,1,0:T(8,128)S(1)} %copy-done.3, f32[64,8,640]{2,1,0:T(8,128)} %copy-done.4, bf16[640,1024]{1,0:T(8,128)(2,1)S(1)} %copy-done, f32[64,8,8,1024]{3,2,1,0:T(8,128)} %get-tuple-element.856, f32[64,8,8]{2,1,0:T(8,128)} %get-tuple-element.851, ...), kind=kOutput, calls=%fused_computation.89 | convolution fusion | flops 5418713088 | bytes 27198464 | tf_op jit(solution)/shard_map/btuv,jv->btuj/dot_general | solution.py:65
  279.5 12.6 %convolution_bitcast_fusion = f32[640,1024]{1,0:T(8,128)} fusion(f32[64,8,640]{2,1,0:T(8,128)S(1)} %copy-done.3, f32[64,8,640]{2,1,0:T(8,128)S(1)} %copy-done.5, f32[64,8,8,1024]{3,2,1,0:T(8,128)S(1)} %bitcast.168, f32[64,8,8]{2,1,0:T(8,128)S(1)} %copy-done.17, f32[64,8,8]{2,1,0:T(8,128)} %copy-done.16, f32[64,8,8]{2,1,0:T(8,128)} %copy-done.15, ...), kind=kOutput, calls=%fused_computation.40 | convolution fusion | flops 5403312128 | bytes 22610944 | tf_op jit(solution)/shard_map/btuj,btuv->jv/dot_general | solution.py:71
  300.9 70.3 %all-reduce.9.cloned.1.call-done = (f32[512,640]{0,1:T(8,128)}, f32[640,640]{0,1:T(8,128)}, f32[640,1024]{1,0:T(8,128)}) async-done(((f32[512,640]{0,1:T(8,128)}, f32[640,640]{0,1:T(8,128)}, f32[640,1024]{1,0:T(8,128)}), (f32[512,640]{0,1:T(8,128)}, f32[640,640]{0,1:T(8,128)}, f32[640,1024]{1,0:T(8,128)})) %all-reduce.9.cloned.1.call-update) | async-done | bytes 5570576 | tf_op jit(solution)/shard_map/psum | solution.py:113
  376.6 3.6 copy.149
  (937 shorter events, 220.9 us)
Async XLA Ops:
  7.2 364.0 %all-reduce.9.cloned.1.call-start = ((), (), s32[]{:S(2)}) async-start(), calls=%async_computation | async-start | bytes 11141120 | tf_op jit(solution)/shard_map/psum | solution.py:113
  46.6 211.7 %copy-start.6 = (f32[64,8,8]{2,1,0:T(8,128)S(1)}, f32[64,8,8]{2,1,0:T(8,128)}, u32[]{:S(2)}) copy-start(f32[64,8,8]{2,1,0:T(8,128)} %get-tuple-element.852) | copy-start | bytes 49156
  50.8 210.3 %copy-start.3 = (f32[64,8,640]{2,1,0:T(8,128)S(1)}, f32[64,8,640]{2,1,0:T(8,128)}, u32[]{:S(2)}) copy-start(f32[64,8,640]{2,1,0:T(8,128)} %copy-done.2) | copy-start | bytes 3932164
  63.3 5.9 %collective-permute-start.1 = (f32[64,8]{0,1:T(8,128)S(1)}, f32[64,8]{0,1:T(8,128)S(1)}, u32[]{:S(2)}, u32[]{:S(2)}) collective-permute-start(f32[64,8]{0,1:T(8,128)S(1)} %get-tuple-element.1100), channel_id=1, source_target_pairs={{1,0},{2,1},{3,2},{4,3},{5,4},{6,5},{7,6},{9,8},{10,9},{11,10},{12... | collective-permute-start | bytes 6152 | tf_op jit(solution)/shard_map/while/body/eval_jaxpr/ppermute | solution.py:103
  81.6 5.0 %collective-permute-start.1 = (f32[64,8]{0,1:T(8,128)S(1)}, f32[64,8]{0,1:T(8,128)S(1)}, u32[]{:S(2)}, u32[]{:S(2)}) collective-permute-start(f32[64,8]{0,1:T(8,128)S(1)} %get-tuple-element.1100), channel_id=1, source_target_pairs={{1,0},{2,1},{3,2},{4,3},{5,4},{6,5},{7,6},{9,8},{10,9},{11,10},{12... | collective-permute-start | bytes 6152 | tf_op jit(solution)/shard_map/while/body/eval_jaxpr/ppermute | solution.py:103
  99.0 5.0 %collective-permute-start.1 = (f32[64,8]{0,1:T(8,128)S(1)}, f32[64,8]{0,1:T(8,128)S(1)}, u32[]{:S(2)}, u32[]{:S(2)}) collective-permute-start(f32[64,8]{0,1:T(8,128)S(1)} %get-tuple-element.1100), channel_id=1, source_target_pairs={{1,0},{2,1},{3,2},{4,3},{5,4},{6,5},{7,6},{9,8},{10,9},{11,10},{12... | collective-permute-start | bytes 6152 | tf_op jit(solution)/shard_map/while/body/eval_jaxpr/ppermute | solution.py:103
  116.4 5.0 %collective-permute-start.1 = (f32[64,8]{0,1:T(8,128)S(1)}, f32[64,8]{0,1:T(8,128)S(1)}, u32[]{:S(2)}, u32[]{:S(2)}) collective-permute-start(f32[64,8]{0,1:T(8,128)S(1)} %get-tuple-element.1100), channel_id=1, source_target_pairs={{1,0},{2,1},{3,2},{4,3},{5,4},{6,5},{7,6},{9,8},{10,9},{11,10},{12... | collective-permute-start | bytes 6152 | tf_op jit(solution)/shard_map/while/body/eval_jaxpr/ppermute | solution.py:103
  133.8 5.0 %collective-permute-start.1 = (f32[64,8]{0,1:T(8,128)S(1)}, f32[64,8]{0,1:T(8,128)S(1)}, u32[]{:S(2)}, u32[]{:S(2)}) collective-permute-start(f32[64,8]{0,1:T(8,128)S(1)} %get-tuple-element.1100), channel_id=1, source_target_pairs={{1,0},{2,1},{3,2},{4,3},{5,4},{6,5},{7,6},{9,8},{10,9},{11,10},{12... | collective-permute-start | bytes 6152 | tf_op jit(solution)/shard_map/while/body/eval_jaxpr/ppermute | solution.py:103
  151.2 5.0 %collective-permute-start.1 = (f32[64,8]{0,1:T(8,128)S(1)}, f32[64,8]{0,1:T(8,128)S(1)}, u32[]{:S(2)}, u32[]{:S(2)}) collective-permute-start(f32[64,8]{0,1:T(8,128)S(1)} %get-tuple-element.1100), channel_id=1, source_target_pairs={{1,0},{2,1},{3,2},{4,3},{5,4},{6,5},{7,6},{9,8},{10,9},{11,10},{12... | collective-permute-start | bytes 6152 | tf_op jit(solution)/shard_map/while/body/eval_jaxpr/ppermute | solution.py:103
  168.6 5.0 %collective-permute-start.1 = (f32[64,8]{0,1:T(8,128)S(1)}, f32[64,8]{0,1:T(8,128)S(1)}, u32[]{:S(2)}, u32[]{:S(2)}) collective-permute-start(f32[64,8]{0,1:T(8,128)S(1)} %get-tuple-element.1100), channel_id=1, source_target_pairs={{1,0},{2,1},{3,2},{4,3},{5,4},{6,5},{7,6},{9,8},{10,9},{11,10},{12... | collective-permute-start | bytes 6152 | tf_op jit(solution)/shard_map/while/body/eval_jaxpr/ppermute | solution.py:103
  202.2 3.8 collective-permute-start
  208.7 4.6 %collective-permute-start = (f32[64,8]{0,1:T(8,128)S(1)}, f32[64,8]{0,1:T(8,128)S(1)}, u32[]{:S(2)}, u32[]{:S(2)}) collective-permute-start(f32[64,8]{0,1:T(8,128)S(1)} %get-tuple-element.1120), channel_id=1, source_target_pairs={{0,1},{1,2},{2,3},{3,4},{4,5},{5,6},{6,7},{8,9},{9,10},{10,11},{11... | collective-permute-start | bytes 6152 | tf_op jit(solution)/shard_map/while/body/eval_jaxpr/ppermute | solution.py:95
  216.1 5.0 %collective-permute-start = (f32[64,8]{0,1:T(8,128)S(1)}, f32[64,8]{0,1:T(8,128)S(1)}, u32[]{:S(2)}, u32[]{:S(2)}) collective-permute-start(f32[64,8]{0,1:T(8,128)S(1)} %get-tuple-element.1120), channel_id=1, source_target_pairs={{0,1},{1,2},{2,3},{3,4},{4,5},{5,6},{6,7},{8,9},{9,10},{10,11},{11... | collective-permute-start | bytes 6152 | tf_op jit(solution)/shard_map/while/body/eval_jaxpr/ppermute | solution.py:95
  223.8 5.0 %collective-permute-start = (f32[64,8]{0,1:T(8,128)S(1)}, f32[64,8]{0,1:T(8,128)S(1)}, u32[]{:S(2)}, u32[]{:S(2)}) collective-permute-start(f32[64,8]{0,1:T(8,128)S(1)} %get-tuple-element.1120), channel_id=1, source_target_pairs={{0,1},{1,2},{2,3},{3,4},{4,5},{5,6},{6,7},{8,9},{9,10},{10,11},{11... | collective-permute-start | bytes 6152 | tf_op jit(solution)/shard_map/while/body/eval_jaxpr/ppermute | solution.py:95
  231.5 5.0 %collective-permute-start = (f32[64,8]{0,1:T(8,128)S(1)}, f32[64,8]{0,1:T(8,128)S(1)}, u32[]{:S(2)}, u32[]{:S(2)}) collective-permute-start(f32[64,8]{0,1:T(8,128)S(1)} %get-tuple-element.1120), channel_id=1, source_target_pairs={{0,1},{1,2},{2,3},{3,4},{4,5},{5,6},{6,7},{8,9},{9,10},{10,11},{11... | collective-permute-start | bytes 6152 | tf_op jit(solution)/shard_map/while/body/eval_jaxpr/ppermute | solution.py:95
  239.2 5.0 %collective-permute-start = (f32[64,8]{0,1:T(8,128)S(1)}, f32[64,8]{0,1:T(8,128)S(1)}, u32[]{:S(2)}, u32[]{:S(2)}) collective-permute-start(f32[64,8]{0,1:T(8,128)S(1)} %get-tuple-element.1120), channel_id=1, source_target_pairs={{0,1},{1,2},{2,3},{3,4},{4,5},{5,6},{6,7},{8,9},{9,10},{10,11},{11... | collective-permute-start | bytes 6152 | tf_op jit(solution)/shard_map/while/body/eval_jaxpr/ppermute | solution.py:95
  246.9 5.0 %collective-permute-start = (f32[64,8]{0,1:T(8,128)S(1)}, f32[64,8]{0,1:T(8,128)S(1)}, u32[]{:S(2)}, u32[]{:S(2)}) collective-permute-start(f32[64,8]{0,1:T(8,128)S(1)} %get-tuple-element.1120), channel_id=1, source_target_pairs={{0,1},{1,2},{2,3},{3,4},{4,5},{5,6},{6,7},{8,9},{9,10},{10,11},{11... | collective-permute-start | bytes 6152 | tf_op jit(solution)/shard_map/while/body/eval_jaxpr/ppermute | solution.py:95
  258.3 21.1 %slice-start = ((s8[16777216]{0:T(1024)(128)(4,1)}), s8[4194304]{0:T(1024)(128)(4,1)S(1)}, s32[]{:S(2)}) async-start(s8[16777216]{0:T(1024)(128)(4,1)} %bitcast.167), calls=%async_computation.1 | async-start | bytes 8388608
  261.1 18.3 %slice-start.1 = ((s8[16777216]{0:T(1024)(128)(4,1)}), s8[4194304]{0:T(1024)(128)(4,1)S(1)}, s32[]{:S(2)}) async-start(s8[16777216]{0:T(1024)(128)(4,1)} %bitcast.167), calls=%async_computation.2 | async-start | bytes 8388608
  261.2 18.3 %slice-start.2 = ((s8[16777216]{0:T(1024)(128)(4,1)}), s8[4194304]{0:T(1024)(128)(4,1)S(1)}, s32[]{:S(2)}) async-start(s8[16777216]{0:T(1024)(128)(4,1)} %bitcast.167), calls=%async_computation.3 | async-start | bytes 8388608
  261.2 18.3 %slice-start.3 = ((s8[16777216]{0:T(1024)(128)(4,1)}), s8[4194304]{0:T(1024)(128)(4,1)S(1)}, s32[]{:S(2)}) async-start(s8[16777216]{0:T(1024)(128)(4,1)} %bitcast.167), calls=%async_computation.4 | async-start | bytes 8388608
  261.2 18.3 %copy-start.5 = (f32[64,8,640]{2,1,0:T(8,128)S(1)}, f32[64,8,640]{2,1,0:T(8,128)}, u32[]{:S(2)}) copy-start(f32[64,8,640]{2,1,0:T(8,128)} %copy-done.4) | copy-start | bytes 3932164
  261.2 18.3 %copy-start.10 = (f32[64,8,8]{2,1,0:T(8,128)S(1)}, f32[64,8,8]{2,1,0:T(8,128)}, u32[]{:S(2)}) copy-start(f32[64,8,8]{2,1,0:T(8,128)} %get-tuple-element.853) | copy-start | bytes 49156
  261.2 18.3 %copy-start.14 = (pred[64,8,1024]{2,1,0:T(8,128)(4,1)S(1)}, pred[64,8,1024]{2,1,0:T(8,128)(4,1)}, u32[]{:S(2)}) copy-start(pred[64,8,1024]{2,1,0:T(8,128)(4,1)} %iota_compare_fusion.2) | copy-start | bytes 1572868
  (21 other events, 171.6 us)
Sparse Core Ops, SparseCore 0:
  298.4 72.7 all-reduce.8
where the time goes:
time: 389 us; the launch traced here: 387 us
  waiting for transfers between devices  97 us (25%)
  other arithmetic  91.7 us (24%)
  local copies, waits for them, and re-layouts  70 us (18%)
  matrix products  54.9 us (14%)
  starting transfers between devices  42.1 us (11%)
  between operations  14.4 us (4%)
  blocking collectives  11.7 us (3%)
  loops' own time  5.3 us (1%)
    psum x1, waiting for transfers between devices, local_fn(): gw_enc, gw_pred, gw_out = lax.psum((gw_enc, gw_pred, gw_out), 'seq')  70.3 us
    dynamic_slice x64, local copies, waits for them, and re-layouts, beta_rows(): lax.scan(frame_step, next_in, (jnp.swapaxes(blank_lp, 0, 1), jnp.swapaxes...  42.4 us
    ge x64, other arithmetic, frame_step(): beta_row = jnp.where((frame_id >= frame_len)[:, None], boundary, beta_row)  40.6 us
    ppermute x7, starting transfers between devices, alpha_hop(): received = lax.ppermute(x_out, 'seq', fwd_pairs)  27.7 us
    ppermute x7, waiting for transfers between devices, beta_hop(): received = lax.ppermute(first_row, 'seq', bwd_pairs)  21.2 us
    dot_general x1, matrix products, joint_backward(): jnp.einsum('btuv,jv->btuj', d_logits, w_out, preferred_element_type=jnp.f...  18.2 us
    unnamed x68, local copies, waits for them, and re-layouts  15.3 us
    ppermute x7, starting transfers between devices, beta_hop(): received = lax.ppermute(first_row, 'seq', bwd_pairs)  14.4 us
  transfers between devices with their start and end apart: 15, of which 15 were waited for; matrix products, arithmetic and copies ran while one was open for 0% of the time, Pallas kernels for 0%

commit v1 on v0

v1 whole, which is shorter than its diff:
```python
import functools

import jax
import jax.numpy as jnp
from jax import lax
from jax.experimental import pallas as pl
from jax.experimental.pallas import tpu as pltpu
from jax.sharding import PartitionSpec as P

NEG = -1.0e30
F32 = jnp.float32
BF16 = jnp.bfloat16
MESH = pl.DeviceIdType.MESH
LANES = 128
NT = (((1,), (1,)), ((), ()))
NN = (((1,), (0,)), ((), ()))
M_D, M_R1L, M_R1R, M_DL, M_DR, M_R2L, M_R2R, M_AL, M_AR, M_OA, M_OB, M_S = range(12)


def mm(a, b, dims=NN):
    return lax.dot_general(a, b, dims, preferred_element_type=F32)


def iota(shape, dim):
    return lax.broadcasted_iota(jnp.int32, shape, dim)


def lae(x, y):
    return jnp.maximum(x, y) + jnp.log(1.0 + jnp.exp(-jnp.abs(x - y)))


def kernel(n, n_utt, n_loc, n_pos,
           f_ref, g_ref, we_ref, wp_ref, wo_ref, meta_ref,
           loss_ref, gf_ref, gwe_ref, gwp_ref, gwo_ref,
           wot, at_s, ct_s, ht, e_s, dz, dhb, dad, pd,
           blank_r, lab_r, rs_r, gb_r, gl_r, sc_r,
           pm, recvp, sp, sr, sa, xb, yb,
           un, recvd, r1, dd, r2, t2, gg,
           lat_s, lat_r, snd, rcv, out_sem):
    me = lax.axis_index("seq")
    nchip = n // 2
    chip, core = me // 2, lax.rem(me, 2)
    k_r, k_l, k_o = lax.rem(chip + 1, nchip), lax.rem(chip + nchip - 1, nchip), lax.rem(chip + 2, nchip)
    right, left, sib = k_r * 2 + core, k_l * 2 + core, me + 1 - 2 * core
    hid = wo_ref.shape[0]
    voc = wo_ref.shape[1]
    enc = f_ref.shape[1]
    n_bt = n_utt * n_loc
    rows_t = n_utt * n_pos
    n_row = n_loc * rows_t

    barrier = pltpu.get_barrier_semaphore()
    for d in range(1, n):
        pl.semaphore_signal(barrier, inc=1, device_id={"seq": lax.rem(me + d, n)}, device_id_type=MESH)

    wot[...] = wo_ref[...].T
    key_r = lax.rem(iota((n_bt, 1), 0), n_loc) * n_utt + iota((n_bt, 1), 0) // n_loc
    col = iota((1, 2 * n_bt), 1)
    key_c = (col // LANES) * n_utt + lax.rem(col, n_utt)
    pd[...] = jnp.where(key_r == key_c, 1.0, 0.0).astype(BF16)
    pc = jnp.where(key_r == iota((1, rows_t), 1), 1.0, 0.0).astype(BF16)
    at = mm(we_ref[...].T, f_ref[...], NT).astype(BF16)
    at_s[...] = mm(at, pd[...])
    ct = mm(wp_ref[...].T, g_ref[...], NT).astype(BF16)
    ct_s[...] = mm(ct, pc)

    fb = rows_t // 2

    def fwd(blk, carry):
        t = blk // 2
        half = lax.rem(blk, 2)
        off = pl.multiple_of(blk * fb, fb)
        hoff = pl.multiple_of(half * fb, fb)
        a = at_s[:, pl.ds(pl.multiple_of(t * LANES, LANES), LANES)]
        c = ct_s[:, pl.ds(hoff, fb)]
        ht[:, pl.ds(off, fb)] = jnp.tanh(jnp.concatenate([a, a], axis=1) + c).astype(BF16)
        e_s[:, pl.ds(off, fb)] = mm(wot[...], ht[:, pl.ds(off, fb)])
        lab = jnp.concatenate([meta_ref[pl.ds(2 * half, 1), :], meta_ref[pl.ds(2 * half + 1, 1), :]], axis=1)
        row8 = iota((8, fb), 0)
        mx = jnp.full((8, fb), NEG, F32)
        lz = jnp.zeros((8, fb), F32)
        for i in range(voc // 8):
            z = e_s[8 * i:8 * i + 8, pl.ds(off, fb)]
            mx = jnp.maximum(mx, z)
            lz = jnp.where(row8 == lab - 8 * i, z, lz)
        z0 = e_s[0:1, pl.ds(off, fb)]
        m = jnp.max(mx, axis=0, keepdims=True)
        lz = jnp.sum(lz, axis=0, keepdims=True)
        mb = jnp.broadcast_to(m, (8, fb))
        s = jnp.zeros((8, fb), F32)
        for i in range(voc // 8):
            e = jnp.exp(e_s[8 * i:8 * i + 8, pl.ds(off, fb)] - mb)
            e_s[8 * i:8 * i + 8, pl.ds(off, fb)] = e
            s = s + e
        s = jnp.sum(s, axis=0, keepdims=True)
        lse = m + jnp.log(s)
        blank_r[pl.ds(t, 1), pl.ds(hoff, fb)] = z0 - lse
        lab_r[pl.ds(t, 1), pl.ds(hoff, fb)] = lz - lse
        rs_r[pl.ds(t, 1), pl.ds(hoff, fb)] = 1.0 / s
        return carry

    lax.fori_loop(0, n_row // fb, fwd, 0)

    lane = iota((n_loc, LANES), 1)
    low = lane < n_utt
    t_loc = iota((n_loc, LANES), 0) + me * n_loc
    t_end = jnp.broadcast_to(meta_ref[4:5, :], (n_loc, LANES))
    live = t_loc < t_end
    for u in range(n_pos):
        q = u // 2
        b = blank_r[:, LANES * q:LANES * (q + 1)]
        l = lab_r[:, LANES * q:LANES * (q + 1)]
        if u == n_pos - 1:
            l = jnp.full((n_loc, LANES), NEG, F32)
        if u % 2 == 0:
            l = pltpu.roll(l, n_utt, 1)
        else:
            b = pltpu.roll(b, n_utt, 1)
        pm[n_loc * u:n_loc * (u + 1), :] = jnp.where(low, jnp.where(live, b, 0.0), jnp.where(live, l, NEG))

    pl.semaphore_wait(barrier, n - 1)

    def lat_copy(d, dst):
        peer = lax.rem(me + d, n)
        return pltpu.make_async_remote_copy(
            src_ref=pm, dst_ref=recvp.at[me if dst else peer], send_sem=lat_s.at[d],
            recv_sem=lat_r.at[me if dst else peer], device_id={"seq": peer}, device_id_type=MESH)

    for d in range(1, n):
        lat_copy(d, True).start()

    fill_lane = iota(sp.shape, 1) < n_utt
    sp[...] = jnp.where(fill_lane, 0.0, NEG)
    sr[...] = jnp.where(fill_lane, NEG, 0.0)
    u_id = iota((n_pos, LANES), 0)
    bound = jnp.where(u_id == jnp.broadcast_to(meta_ref[5:6, :], (n_pos, LANES)), 0.0, NEG)
    init = jnp.where(u_id == 0, 0.0, NEG)

    def put(rows, src):
        for u in range(n_pos):
            x = src[n_loc * u:n_loc * (u + 1), :]
            base = rows + (n_pos + 1) * u
            sp[pl.ds(base, n_loc, stride=n_pos), :] = x
            sr[pl.ds(base, n_loc, stride=n_pos), :] = pltpu.roll(x, n_utt, 1)

    put(me * (n_loc * n_pos), pm)
    for d in range(1, n):
        peer = lax.rem(me + d, n)
        lat_copy(d, False).wait_recv()
        put(peer * (n_loc * n_pos), recvp.at[peer])

    n_diag = n * n_loc + n_pos - 1

    def lattice(step, carry):
        s_a, s_b = carry
        da = pl.multiple_of(step * n_pos, n_pos)
        db = pl.multiple_of((n_diag - 1 - step) * n_pos, n_pos)
        sa[pl.ds(da, n_pos), :] = s_a
        x_a = s_a + sp[pl.ds(da, n_pos), :]
        y_a = pltpu.roll(s_a + sr[pl.ds(da, n_pos), :], 1, 0)
        x_b = s_b + sp[pl.ds(db, n_pos), :]
        y_b = pltpu.roll(s_b, n_pos - 1, 0) + sr[pl.ds(db, n_pos), :]
        xb[pl.ds(db, n_pos), :] = x_b
        yb[pl.ds(db, n_pos), :] = y_b
        return lae(x_a, y_a), lae(x_b, y_b)

    _, s_b = lax.fori_loop(0, n_diag, lattice, (init, bound))
    logp = s_b[0:1, :]
    loss_ref[...] = jnp.broadcast_to(-logp, loss_ref.shape)
    lp8 = jnp.broadcast_to(logp, (n_loc, LANES))

    gbs, gls = [], []
    for u in range(n_pos):
        rows = pl.ds(me * (n_loc * n_pos) + (n_pos + 1) * u, n_loc, stride=n_pos)
        al = sa[rows, :] - lp8
        gbs.append(jnp.where(live, jnp.exp(jnp.minimum(al + xb[rows, :], 0.0)), 0.0))
        gls.append(jnp.where(live, jnp.exp(jnp.minimum(al + yb[rows, :], 0.0)), 0.0))
    for q in range(n_pos // 2):
        ls = slice(LANES * q, LANES * (q + 1))
        gb = jnp.where(low, gbs[2 * q], pltpu.roll(gbs[2 * q + 1], n_utt, 1))
        gl = jnp.where(low, gls[2 * q], pltpu.roll(gls[2 * q + 1], n_utt, 1))
        gb_r[:, ls] = gb
        gl_r[:, ls] = gl
        sc_r[:, ls] = (gb + gl) * rs_r[:, ls]

    u_rows = un.shape[1]
    h_rows = u_rows // 2
    p_rows = h_rows // nchip
    s_rows = p_rows // 2
    mine = core * h_rows

    def msg(kind, i, src, dst, dev):
        return pltpu.make_async_remote_copy(
            src_ref=src, dst_ref=dst, send_sem=snd.at[kind, i], recv_sem=rcv.at[kind, i],
            device_id={"seq": dev}, device_id_type=MESH)

    sent = []

    def send(*args):
        m = msg(*args)
        m.start()
        sent.append(m)

    def take(kind, i, ref):
        msg(kind, i, ref, ref, sib).wait_recv()

    def hp(i, k, lo, size):
        return un.at[i, pl.ds(mine + k * p_rows + lo, size)]

    def gp(i, k, lo, size):
        return gg.at[i, pl.ds(mine + k * p_rows + lo, size)]

    def step0(i):
        send(M_D, i, un.at[i, pl.ds((1 - core) * h_rows, h_rows)], recvd.at[i], sib)

    def step1(i):
        take(M_D, i, recvd.at[i])
        un[i, pl.ds(mine, h_rows)] += recvd[i]
        send(M_R1L, i, hp(i, k_o, 0, s_rows), r1.at[i, 0], right)
        send(M_R1R, i, hp(i, k_o, s_rows, s_rows), r1.at[i, 1], left)
        send(M_DL, i, hp(i, k_r, s_rows, s_rows), dd.at[i, 0], right)
        send(M_DR, i, hp(i, k_l, 0, s_rows), dd.at[i, 1], left)

    def step2(i):
        take(M_R1L, i, r1.at[i, 0])
        t2[i, 0] = hp(i, k_r, 0, s_rows)[...] + r1[i, 0]
        send(M_R2L, i, t2.at[i, 0], r2.at[i, 0], right)
        take(M_R1R, i, r1.at[i, 1])
        t2[i, 1] = hp(i, k_l, s_rows, s_rows)[...] + r1[i, 1]
        send(M_R2R, i, t2.at[i, 1], r2.at[i, 1], left)

    def step3(i):
        take(M_DR, i, dd.at[i, 1])
        take(M_R2L, i, r2.at[i, 0])
        gg[i, pl.ds(mine + chip * p_rows, s_rows)] = hp(i, chip, 0, s_rows)[...] + r2[i, 0] + dd[i, 1]
        take(M_DL, i, dd.at[i, 0])
        take(M_R2R, i, r2.at[i, 1])
        gg[i, pl.ds(mine + chip * p_rows + s_rows, s_rows)] = hp(i, chip, s_rows, s_rows)[...] + r2[i, 1] + dd[i, 0]
        own = gp(i, chip, 0, p_rows)
        send(M_AL, i, own, own, right)
        send(M_AR, i, own, own, left)

    def step4(i):
        take(M_AL, i, gp(i, k_l, 0, p_rows))
        send(M_OA, i, gp(i, k_l, 0, s_rows), gp(i, k_l, 0, s_rows), right)
        take(M_AR, i, gp(i, k_r, 0, p_rows))
        send(M_OB, i, gp(i, k_r, s_rows, s_rows), gp(i, k_r, s_rows, s_rows), left)

    def step5(i):
        take(M_OA, i, gp(i, k_o, 0, s_rows))
        take(M_OB, i, gp(i, k_o, s_rows, s_rows))
        half = gg.at[i, pl.ds(mine, h_rows)]
        send(M_S, i, half, half, sib)

    outs = []

    def step6(i):
        take(M_S, i, gg.at[i, pl.ds((1 - core) * h_rows, h_rows)])
        if i < 4:
            for s in range(2):
                cols = slice((2 * i + s) * LANES, (2 * i + s + 1) * LANES)
                cp = pltpu.make_async_copy(gg.at[i, pl.ds(s * hid, hid)], gwo_ref.at[:, cols], out_sem.at[i, s])
                cp.start()
                outs.append(cp)
        elif i == 7:
            n_blk = hid // LANES
            for s in range(n_blk):
                cols = slice(s * LANES, (s + 1) * LANES)
                lo, hi = s * enc, (s + 1) * enc
                first = lo
                while first < hi:
                    unit = first // u_rows
                    last = min(hi, (unit + 1) * u_rows)
                    cp = pltpu.make_async_copy(
                        gg.at[6 + unit, pl.ds(first - unit * u_rows, last - first)],
                        gwe_ref.at[pl.ds(first - lo, last - first), cols], out_sem.at[4 + unit, s])
                    cp.start()
                    outs.append(cp)
                    first = last

    steps = (step0, step1, step2, step3, step4, step5, step6)
    done = [0] * 8

    def advance(*units):
        for i in units:
            steps[done[i]](i)
            done[i] += 1

    vb = u_rows // hid * LANES

    def make_dz(i):
        def per_t(t, carry):
            off = pl.multiple_of(t * rows_t, rows_t)
            sc = sc_r[pl.ds(t, 1), :]
            gl = gl_r[pl.ds(t, 1), :]
            lab = jnp.concatenate([meta_ref[q:q + 1, :] for q in range(4)], axis=1)
            scb = jnp.broadcast_to(sc, (16, rows_t))
            glb = jnp.broadcast_to(gl, (16, rows_t))
            row = iota((16, rows_t), 0)

            def grp(j, c2):
                r0 = pl.multiple_of(i * vb + j * 16, 16)
                x = e_s[pl.ds(r0, 16), pl.ds(off, rows_t)] * scb
                x = jnp.where(row == lab - r0, x - glb, x)
                dz[pl.ds(r0, 16), pl.ds(off, rows_t)] = x.astype(BF16)
                return c2

            lax.fori_loop(0, vb // 16, grp, 0)
            if i == 0:
                gb = gb_r[pl.ds(t, 1), :]
                x = e_s[0:16, pl.ds(off, rows_t)] * scb
                x = jnp.where(row == lab, x - glb, x)
                x = jnp.where(row == 0, x - jnp.broadcast_to(gb, (16, rows_t)), x)
                dz[0:16, pl.ds(off, rows_t)] = x.astype(BF16)
            return carry

        lax.fori_loop(0, n_loc, per_t, 0)

    def make_out(i):
        un[i] = jnp.zeros((u_rows, LANES), F32)
        kc = n_row // 4

        def chunk(r, carry):
            lo = pl.multiple_of(r * kc, kc)
            x = mm(ht[:, pl.ds(lo, kc)], dz[i * vb:(i + 1) * vb, pl.ds(lo, kc)], NT)
            un[i, 0:hid] += x[:, 0:LANES]
            un[i, hid:2 * hid] += x[:, LANES:2 * LANES]
            return carry

        lax.fori_loop(0, 4, chunk, 0)

    for i in range(4):
        make_dz(i)
        make_out(i)
        advance(i)
        for j in range(i - 1, -1, -1):
            advance(j)

    un[4:6] = jnp.zeros((2, u_rows, LANES), F32)

    def back(t, carry):
        off = pl.multiple_of(t * rows_t, rows_t)
        dhb[...] = mm(wo_ref[...], dz[:, pl.ds(off, rows_t)])
        for i in range(hid // 16):
            rr = slice(16 * i, 16 * i + 16)
            h = ht[rr, pl.ds(off, rows_t)].astype(F32)
            dp = (dhb[rr, :] * (1.0 - h * h)).astype(BF16).astype(F32)
            x = None
            for q in range(rows_t // LANES):
                y = dp[:, q * LANES:(q + 1) * LANES]
                lo = q % 2 * hid + 16 * i
                un[4 + q // 2, lo:lo + 16] += y
                x = y if x is None else x + y
            x = x + pltpu.roll(x, n_utt, 1)
            x = jnp.where(iota((16, LANES), 1) < n_utt, x, 0.0)
            dad[rr, pl.ds(pl.multiple_of(t * LANES, LANES), LANES)] = x.astype(BF16)
        return carry

    for part in range(4):
        lax.fori_loop(part * n_loc // 4, (part + 1) * n_loc // 4, back, 0)
        for j in range(4):
            if done[j] < 7:
                advance(j)

    for i in range(2):
        advance(4 + i)
    da = mm(pd[...], dad[...], NT).astype(BF16)
    advance(4, 5)
    x = mm(f_ref[...].T, da)
    for s in range(hid // LANES):
        lo, hi = s * enc, (s + 1) * enc
        first = lo
        while first < hi:
            unit = first // u_rows
            last = min(hi, (unit + 1) * u_rows)
            un[6 + unit, first - unit * u_rows:last - unit * u_rows] = x[first - lo:last - lo, s * LANES:(s + 1) * LANES]
            first = last
    advance(6, 7)
    gf_ref[...] = mm(da, we_ref[...], NT).astype(BF16)
    gpt = mm(g_ref[...].T, pc).astype(BF16)
    while min(done) < 7:
        order = sorted(range(8), key=lambda j: (-done[j], j))
        for j in order:
            if done[j] < 7:
                advance(j)
    dcb = jnp.concatenate([gg[4, 0:hid], gg[4, hid:2 * hid], gg[5, 0:hid], gg[5, hid:2 * hid]], axis=1).astype(BF16)
    gwp_ref[...] = mm(gpt, dcb, NT)
    for m in sent:
        m.wait_send()
    for d in range(1, n):
        lat_copy(d, True).wait_send()
    for cp in outs:
        cp.wait()


def solution(mesh):
    n = mesh.shape["seq"]

    def local_fn(enc_out, pred_out, w_enc, w_pred, w_out, labels, frame_len, label_len):
        n_utt, n_loc, enc = enc_out.shape
        n_pos, pred = pred_out.shape[1:]
        hid, voc = w_out.shape
        assert n == 8 and 2 * n_utt == LANES and n_loc == 8 and n_pos == 8
        n_bt = n_utt * n_loc
        rows_t = n_utt * n_pos
        n_row = n_loc * rows_t
        lab = jnp.concatenate([labels.T, jnp.full((1, n_utt), -1, jnp.int32)], axis=0).reshape(n_pos // 2, LANES)
        lens = jnp.stack([frame_len, label_len])
        lens = jnp.concatenate([lens, lens], axis=1)
        meta = jnp.concatenate([lab, lens, jnp.zeros((2, LANES), jnp.int32)], axis=0)
        u_rows = 2 * hid
        h_rows = u_rows // 2
        s_rows = h_rows // n
        vm = pl.BlockSpec(memory_space=pltpu.VMEM)
        anys = pl.BlockSpec(memory_space=pl.ANY)
        n_sk = (n * n_loc + n_pos) * n_pos
        scratch = [
            pltpu.VMEM((voc, hid), BF16),
            pltpu.VMEM((hid, n_loc * LANES), F32),
            pltpu.VMEM((hid, rows_t), F32),
            pltpu.VMEM((hid, n_row), BF16),
            pltpu.VMEM((voc, n_row), F32),
            pltpu.VMEM((voc, n_row), BF16),
            pltpu.VMEM((hid, rows_t), F32),
            pltpu.VMEM((hid, n_loc * LANES), BF16),
            pltpu.VMEM((n_bt, n_loc * LANES), BF16),
        ] + [pltpu.VMEM((n_loc, rows_t), F32)] * 6 + [
            pltpu.VMEM((n_loc * n_pos, LANES), F32),
            pltpu.VMEM((n, n_loc * n_pos, LANES), F32),
        ] + [pltpu.VMEM((n_sk, LANES), F32)] * 5 + [
            pltpu.VMEM((8, u_rows, LANES), F32),
            pltpu.VMEM((8, h_rows, LANES), F32),
            pltpu.VMEM((8, 2, s_rows, LANES), F32),
            pltpu.VMEM((8, 2, s_rows, LANES), F32),
            pltpu.VMEM((8, 2, s_rows, LANES), F32),
            pltpu.VMEM((8, 2, s_rows, LANES), F32),
            pltpu.VMEM((8, u_rows, LANES), F32),
            pltpu.SemaphoreType.DMA((n,)),
            pltpu.SemaphoreType.DMA((n,)),
            pltpu.SemaphoreType.DMA((12, 8)),
            pltpu.SemaphoreType.DMA((12, 8)),
            pltpu.SemaphoreType.DMA((6, 5)),
        ]
        loss, gf, gwe, gwp, gwo = pl.pallas_call(
            functools.partial(kernel, n, n_utt, n_loc, n_pos),
            out_shape=(
                jax.ShapeDtypeStruct((8, LANES), F32),
                jax.ShapeDtypeStruct((n_bt, enc), BF16),
                jax.ShapeDtypeStruct((enc, hid), F32),
                jax.ShapeDtypeStruct((pred, hid), F32),
                jax.ShapeDtypeStruct((hid, voc), F32),
            ),
            in_specs=[vm] * 6,
            out_specs=(vm, vm, anys, vm, anys),
            scratch_shapes=scratch,
            compiler_params=pltpu.CompilerParams(collective_id=0, has_side_effects=True, vmem_limit_bytes=67043328),
            name="rnnt",
        )(enc_out.reshape(n_bt, enc), pred_out.reshape(n_utt * n_pos, pred), w_enc, w_pred, w_out, meta)
        return loss[0, :n_utt], gf.reshape(n_utt, n_loc, enc), gwe, gwp, gwo

    in_specs = (P("dp", "seq", None), P("dp", None, None), P(None, None), P(None, None), P(None, None), P("dp", None), P("dp"), P("dp"))
    out_specs = (P("dp"), P("dp", "seq", None), P("dp", None), P("dp", None), P("dp", None))
    return jax.shard_map(local_fn, mesh=mesh, in_specs=in_specs, out_specs=out_specs, check_vma=False)
```

time: 389 us -> 112 us (0.29)
  Pallas kernels: 0 us -> 99.7 us
  waiting for transfers between devices: 97 us -> 0 us
  other arithmetic: 91.7 us -> 1.41 us
  local copies, waits for them, and re-layouts: 70 us -> 10.3 us
  matrix products: 54.9 us -> 0 us
  starting transfers between devices: 42.1 us -> 0 us
  between operations: 14.4 us -> 0.65 us
  blocking collectives: 11.7 us -> 0 us
  loops' own time: 5.3 us -> 0 us
    pallas_call x0 -> x1, Pallas kernels: none -> 99.7 us  [local_fn(): pl.pallas_call(functools.partial(kernel, n, n_utt, n_loc, n_pos), out_sha...]
    psum x1 -> x0, waiting for transfers between devices: 70.3 us -> none  [local_fn(): gw_enc, gw_pred, gw_out = lax.psum((gw_enc, gw_pred, gw_out), 'seq')]
    dot_general x10 -> x0, matrix products: 54.9 us -> none  [the longest x1 18.2 us: joint_backward(): jnp.einsum('btuv,jv->btuj', d_logits, w_out, preferred_element_type=jnp.f...]
    dynamic_slice x64 -> x0, local copies, waits for them, and re-layouts: 42.4 us -> none  [beta_rows(): lax.scan(frame_step, next_in, (jnp.swapaxes(blank_lp, 0, 1), jnp.swapaxes...]
    ppermute x14 -> x0, starting transfers between devices: 42 us -> none  [the longest x7 27.7 us: alpha_hop(): received = lax.ppermute(x_out, 'seq', fwd_pairs)]
    ge x64 -> x0, other arithmetic: 40.6 us -> none  [frame_step(): beta_row = jnp.where((frame_id >= frame_len)[:, None], boundary, beta_row)]
    ppermute x14 -> x0, waiting for transfers between devices: 26.7 us -> none  [the longest x7 21.2 us: beta_hop(): received = lax.ppermute(first_row, 'seq', bwd_pairs)]
    another operation x256 -> x0, other arithmetic: 24.6 us -> none  [the longest x64 10.9 us: frame_step(): lax.cumlogsumexp(next_row + frame_blank + lab_sum, axis=1, reverse=True)]
  transfers between devices with their start and end apart: 15 -> 0, of which waited for: 15 -> 0; matrix products, arithmetic and copies ran while one was open for 0% -> 0% of each run, Pallas kernels for 0% -> 0%
where the time goes in v1:
time: 112 us
  Pallas kernels  99.7 us (89%)
  local copies, waits for them, and re-layouts  10.3 us (9%)
  other arithmetic  1.41 us (1%)
    pallas_call x1, Pallas kernels, local_fn(): pl.pallas_call(functools.partial(kernel, n, n_utt, n_loc, n_pos), out_sha...  99.7 us
    unnamed x8, local copies, waits for them, and re-layouts  8.27 us

profile of v1, /device:TPU:113, one launch (start us, length us, event | category | flops | bytes accessed | tf_op | source)
XLA Modules:
  0.0 112.0 jit_solution(6932737232057469037)
XLA Ops:
  0.6 0.1 pad.6.clone
  0.7 0.7 concatenate.9
  1.4 0.1 reshape.24
  1.5 1.4 %add_add_fusion.meta_ref = s32[8,128]{1,0:T(8,128)} fusion(s32[1,64]{1,0:T(1,128)} %bitcast.12, s32[1,64]{1,0:T(1,128)} %bitcast.13, s32[4,128]{1,0:T(4,128)S(1)} %reshape.24, s32[8]{0:T(128)S(1)} %pad.6.clone), kind=kLoop, calls=%fused_computation | loop fusion | flops 5120 | bytes 6688 | tf_op jit(solution)/shard_map/concatenate | solution.py:410
  2.9 99.7 %rnnt.1 = (f32[8,128]{1,0:T(8,128)}, bf16[512,512]{1,0:T(8,128)(2,1)}, f32[512,640]{1,0:T(8,128)}, f32[640,640]{1,0:T(8,128)}, f32[640,1024]{1,0:T(8,128)}) custom-call(bf16[512,512]{1,0:T(8,128)(2,1)} %bitcast.9, bf16[512,640]{1,0:T(8,128)(2,1)} %bitcast.8, bf16[512,640]{1,0:T(8,128)(2,1)} %we_ref.1, bf16[640,640]{1,0:T(8,128)(2,1)} %wp_ref.1, ...), custom_call_target="tpu_custom_call" | custom-call | tf_op jit(solution)/shard_map/rnnt/pallas_call | solution.py:444
  102.6 1.2 %slice_bitcast_fusion = f32[64]{0:T(128)} fusion(f32[8,128]{1,0:T(8,128)} %get-tuple-element.10), kind=kLoop, calls=%fused_computation.1 | loop fusion | bytes 512 | tf_op jit(solution)/shard_map/squeeze | solution.py:459
  103.8 0.0 copy-start.1
  103.8 2.0 %copy.17 = bf16[64,8,512]{2,1,0:T(8,128)(2,1)} copy(bf16[64,8,512]{2,1,0:T(8,128)(2,1)} %bitcast.10) | data formatting | bytes 1048576
  105.8 2.5 %copy.18 = f32[512,640]{1,0:T(8,128)} copy(f32[512,640]{1,0:T(8,128)} %get-tuple-element.22) | data formatting | bytes 2621440
  108.2 0.0 copy-done.1
  108.2 0.0 copy-start
  108.2 1.2 %copy.19 = f32[640,640]{1,0:T(8,128)} copy(f32[640,640]{1,0:T(8,128)S(1)} %copy-done.1) | data formatting | bytes 3276800
  109.4 1.2 %copy-done = f32[640,1024]{1,0:T(8,128)S(1)} copy-done((f32[640,1024]{1,0:T(8,128)S(1)}, f32[640,1024]{1,0:T(8,128)}, u32[]{:S(2)}) %copy-start) | copy-done | bytes 2621464
  110.5 1.5 %copy.20 = f32[640,1024]{1,0:T(8,128)} copy(f32[640,1024]{1,0:T(8,128)S(1)} %copy-done) | data formatting | bytes 5242880
  (1 shorter events, 0.0 us)
Async XLA Ops:
  103.8 4.5 %copy-start.1 = (f32[640,640]{1,0:T(8,128)S(1)}, f32[640,640]{1,0:T(8,128)}, u32[]{:S(2)}) copy-start(f32[640,640]{1,0:T(8,128)} %get-tuple-element.23) | copy-start | bytes 4915204
  108.2 2.3 %copy-start = (f32[640,1024]{1,0:T(8,128)S(1)}, f32[640,1024]{1,0:T(8,128)}, u32[]{:S(2)}) copy-start(f32[640,1024]{1,0:T(8,128)} %get-tuple-element.24) | copy-start | bytes 7864324

commit v2 on v1

v2 whole, which is shorter than its diff:
```python
import functools

import jax
import jax.numpy as jnp
from jax import lax
from jax.experimental import pallas as pl
from jax.experimental.pallas import tpu as pltpu
from jax.sharding import PartitionSpec as P

NEG = -1.0e30
F32 = jnp.float32
BF16 = jnp.bfloat16
MESH = pl.DeviceIdType.MESH
LANES = 128
VMEM_LIMIT = 57 * 2 ** 20
NT = (((1,), (1,)), ((), ()))
NN = (((1,), (0,)), ((), ()))
M_D, M_R1L, M_R1R, M_DL, M_DR, M_R2L, M_R2R, M_AL, M_AR, M_OA, M_OB, M_S = range(12)


def mm(a, b, dims=NN):
    return lax.dot_general(a, b, dims, preferred_element_type=F32)


def iota(shape, dim):
    return lax.broadcasted_iota(jnp.int32, shape, dim)


def lae(x, y):
    return jnp.maximum(x, y) + jnp.log(1.0 + jnp.exp(-jnp.abs(x - y)))


LINK_RATE, LINK_LAT, CORE_RATE, CORE_LAT = 46.6e3, 1.9, 600e3, 1.1
NEEDS = ((), (M_D,), (M_R1L, M_R1R), (M_DL, M_DR, M_R2L, M_R2R), (M_AL, M_AR), (M_OA, M_OB), (M_S,))
COSTS = (.02, .25, .1, .2, .05, .05, .05)


def static_order(segs, piece, narrow):
    now, free, arrive, done, order, made = 0.0, {}, {}, {}, [], []

    def tx(kind, u, link, size):
        rate, lat = (CORE_RATE, CORE_LAT) if link == "c" else (LINK_RATE, LINK_LAT)
        begin = max(now, free.get(link, 0.0))
        free[link] = begin + size / rate
        arrive[kind, u] = free[link] + lat

    def ready(u):
        return max([arrive[k, u] for k in NEEDS[done[u]]], default=0.0)

    def step(u):
        nonlocal now
        k = done[u]
        now = max(now, ready(u)) + COSTS[k]
        ag = piece / 2 if u in narrow else piece
        if k == 0:
            tx(M_D, u, "c", 4 * piece)
        elif k == 1:
            for kind, link in ((M_R1L, "r"), (M_R1R, "l"), (M_DL, "r"), (M_DR, "l")):
                tx(kind, u, link, piece / 2)
        elif k == 2:
            tx(M_R2L, u, "r", piece / 2)
            tx(M_R2R, u, "l", piece / 2)
        elif k == 3:
            tx(M_AL, u, "r", ag)
            tx(M_AR, u, "l", ag)
        elif k == 4:
            tx(M_OA, u, "r", ag / 2)
            tx(M_OB, u, "l", ag / 2)
        elif k == 5:
            tx(M_S, u, "c", 4 * ag)
        done[u] += 1
        order.append((1, u))

    left = list(range(len(segs)))
    while True:
        cand = [u for u in made if done[u] < 7]
        now_ready = [u for u in cand if ready(u) <= now]
        if now_ready:
            step(min(now_ready, key=lambda u: (done[u] > 3, made.index(u))))
        elif left:
            i = left.pop(0)
            order.append((0, i))
            now += segs[i][0]
            for u in segs[i][2]:
                made.append(u)
                done[u] = 0
        elif cand:
            step(min(cand, key=ready))
        else:
            return order


def kernel(n, n_utt, n_loc, n_pos,
           f_ref, g_ref, we_ref, wp_ref, wo_ref, lab_ref, flen_ref, llen_ref,
           loss_ref, gf_ref, gg, gd, gpt_ref,
           wot, at_s, ct_s, ht, e_s, za, zc, dz0, dz1, dz2, dz3, dad, dacc, pd, trs, lab_s, len_s,
           blank_r, lab_r, rs_r, gb_r, gl_r, sc_r,
           pm, recvp, sp, sr, sa, xb, yb,
           un, recvd, r1, dd, r2, t2,
           lat_s, lat_r, snd, rcv):
    me = lax.axis_index("seq")
    nchip = n // 2
    chip, core = me // 2, lax.rem(me, 2)
    k_r, k_l, k_o = lax.rem(chip + 1, nchip), lax.rem(chip + nchip - 1, nchip), lax.rem(chip + 2, nchip)
    right, left, sib = k_r * 2 + core, k_l * 2 + core, me + 1 - 2 * core
    hid = wo_ref.shape[0]
    voc = wo_ref.shape[1]
    enc = f_ref.shape[1]
    n_bt = n_utt * n_loc
    rows_t = n_utt * n_pos
    n_row = n_loc * rows_t

    barrier = pltpu.get_barrier_semaphore()
    for d in range(1, n):
        pl.semaphore_signal(barrier, inc=1, device_id={"seq": lax.rem(me + d, n)}, device_id_type=MESH)

    wot[...] = wo_ref[...].T
    trs[...] = jnp.full(trs.shape, -1, jnp.int32)
    trs[0:n_pos - 1, 0:n_utt] = lab_ref[...]
    lab_t = trs[...]
    lab_alt = pltpu.roll(lab_t, n_utt, 1)
    low1 = iota((1, LANES), 1) < n_utt
    for q in range(n_pos // 2):
        lab_s[0:1, LANES * q:LANES * (q + 1)] = jnp.where(low1, lab_t[2 * q:2 * q + 1], lab_alt[2 * q + 1:2 * q + 2])
    len_s[0:1, 0:n_utt] = flen_ref[...]
    len_s[1:2, 0:n_utt] = llen_ref[...]
    key_r = lax.rem(iota((n_bt, 1), 0), n_loc) * n_utt + iota((n_bt, 1), 0) // n_loc
    col = iota((1, 2 * n_bt), 1)
    key_c = (col // LANES) * n_utt + lax.rem(col, n_utt)
    pd[...] = jnp.where(key_r == key_c, 1.0, 0.0).astype(BF16)
    pc = jnp.where(key_r == iota((1, rows_t), 1), 1.0, 0.0).astype(BF16)
    at = mm(we_ref[...].T, f_ref[...], NT).astype(BF16)
    at_s[...] = mm(at, pd[...]).astype(BF16)
    ct = mm(wp_ref[...].T, g_ref[...], NT).astype(BF16)
    ct_s[...] = mm(ct, pc).astype(BF16)
    gpt_ref[...] = mm(g_ref[...].T, pc).astype(BF16)

    fb = rows_t // 2
    n_blk = n_row // fb

    def logits(blk, z_ref):
        t = blk // 2
        off = pl.multiple_of(blk * fb, fb)
        a = at_s[:, pl.ds(pl.multiple_of(t * LANES, LANES), LANES)].astype(F32)
        c = ct_s[:, pl.ds(pl.multiple_of(lax.rem(blk, 2) * fb, fb), fb)].astype(F32)
        h = jnp.tanh(jnp.concatenate([a, a], axis=1) + c).astype(BF16)
        ht[:, pl.ds(off, fb)] = h
        z_ref[...] = mm(wot[...], h)

    def norm(blk, z_ref):
        t = blk // 2
        off = pl.multiple_of(blk * fb, fb)
        hoff = pl.multiple_of(lax.rem(blk, 2) * fb, fb)
        lab = lab_s[0:1, pl.ds(hoff, fb)]
        ch = LANES
        row = iota((ch, fb), 0)
        mx = jnp.full((8, fb), NEG, F32)
        lz = jnp.zeros((8, fb), F32)
        for i in range(voc // ch):
            z = z_ref[ch * i:ch * (i + 1), :]
            hit = jnp.where(row == lab - ch * i, z, 0.0)
            mx = jnp.maximum(mx, jnp.max(z.reshape(ch // 8, 8, fb), axis=0))
            lz = lz + jnp.sum(hit.reshape(ch // 8, 8, fb), axis=0)
        m = jnp.max(mx, axis=0, keepdims=True)
        lz = jnp.sum(lz, axis=0, keepdims=True)
        s = jnp.zeros((8, fb), F32)
        for i in range(voc // ch):
            e = jnp.exp(z_ref[ch * i:ch * (i + 1), :] - m)
            e_s[ch * i:ch * (i + 1), pl.ds(off, fb)] = e
            s = s + jnp.sum(e.reshape(ch // 8, 8, fb), axis=0)
        s = jnp.sum(s, axis=0, keepdims=True)
        lse = m + jnp.log(s)
        blank_r[pl.ds(t, 1), pl.ds(hoff, fb)] = z_ref[0:1, :] - lse
        lab_r[pl.ds(t, 1), pl.ds(hoff, fb)] = lz - lse
        rs_r[pl.ds(t, 1), pl.ds(hoff, fb)] = 1.0 / s

    def fwd(j, carry):
        logits(2 * j + 1, zc)
        norm(2 * j, za)
        logits(2 * j + 2, za)
        norm(2 * j + 1, zc)
        return carry

    logits(0, za)
    lax.fori_loop(0, n_blk // 2 - 1, fwd, 0)
    logits(n_blk - 1, zc)
    norm(n_blk - 2, za)
    norm(n_blk - 1, zc)

    lane = iota((n_loc, LANES), 1)
    low = lane < n_utt
    t_loc = iota((n_loc, LANES), 0) + me * n_loc
    len2 = jnp.where(low1, len_s[0:1, :], pltpu.roll(len_s[0:1, :], n_utt, 1))
    t_end = jnp.broadcast_to(len2, (n_loc, LANES))
    live = t_loc < t_end
    for u in range(n_pos):
        q = u // 2
        b = blank_r[:, LANES * q:LANES * (q + 1)]
        l = lab_r[:, LANES * q:LANES * (q + 1)]
        if u == n_pos - 1:
            l = jnp.full((n_loc, LANES), NEG, F32)
        if u % 2 == 0:
            l = pltpu.roll(l, n_utt, 1)
        else:
            b = pltpu.roll(b, n_utt, 1)
        pm[n_loc * u:n_loc * (u + 1), :] = jnp.where(low, jnp.where(live, b, 0.0), jnp.where(live, l, NEG))

    pl.semaphore_wait(barrier, n - 1)

    def lat_copy(d, dst):
        peer = lax.rem(me + d, n)
        return pltpu.make_async_remote_copy(
            src_ref=pm, dst_ref=recvp.at[me if dst else peer], send_sem=lat_s.at[d],
            recv_sem=lat_r.at[me if dst else peer], device_id={"seq": peer}, device_id_type=MESH)

    for d in range(1, n):
        lat_copy(d, True).start()

    fill_lane = iota(sp.shape, 1) < n_utt
    sp[...] = jnp.where(fill_lane, 0.0, NEG)
    sr[...] = jnp.where(fill_lane, NEG, 0.0)
    u_id = iota((n_pos, LANES), 0)
    bound = jnp.where(u_id == jnp.broadcast_to(len_s[1:2, :], (n_pos, LANES)), 0.0, NEG)
    init = jnp.where(u_id == 0, 0.0, NEG)

    def put(rows, src):
        for u in range(n_pos):
            x = src[n_loc * u:n_loc * (u + 1), :]
            base = rows + (n_pos + 1) * u
            sp[pl.ds(base, n_loc, stride=n_pos), :] = x
            sr[pl.ds(base, n_loc, stride=n_pos), :] = pltpu.roll(x, n_utt, 1)

    put(me * (n_loc * n_pos), pm)
    for d in range(1, n):
        peer = lax.rem(me + d, n)
        lat_copy(d, False).wait_recv()
        put(peer * (n_loc * n_pos), recvp.at[peer])

    n_diag = n * n_loc + n_pos - 1

    def lattice(step, carry):
        s_a, s_b = carry
        da = pl.multiple_of(step * n_pos, n_pos)
        db = pl.multiple_of((n_diag - 1 - step) * n_pos, n_pos)
        sa[pl.ds(da, n_pos), :] = s_a
        x_a = s_a + sp[pl.ds(da, n_pos), :]
        y_a = pltpu.roll(s_a + sr[pl.ds(da, n_pos), :], 1, 0)
        x_b = s_b + sp[pl.ds(db, n_pos), :]
        y_b = pltpu.roll(s_b, n_pos - 1, 0) + sr[pl.ds(db, n_pos), :]
        xb[pl.ds(db, n_pos), :] = x_b
        yb[pl.ds(db, n_pos), :] = y_b
        return lae(x_a, y_a), lae(x_b, y_b)

    _, s_b = lax.fori_loop(0, n_diag, lattice, (init, bound))
    logp = s_b[0:1, :]
    loss_ref[...] = jnp.broadcast_to(-logp, loss_ref.shape)
    lp8 = jnp.broadcast_to(logp, (n_loc, LANES))

    gbs, gls = [], []
    for u in range(n_pos):
        rows = pl.ds(me * (n_loc * n_pos) + (n_pos + 1) * u, n_loc, stride=n_pos)
        al = sa[rows, :] - lp8
        gbs.append(jnp.where(live, jnp.exp(jnp.minimum(al + xb[rows, :], 0.0)), 0.0))
        gls.append(jnp.where(live, jnp.exp(jnp.minimum(al + yb[rows, :], 0.0)), 0.0))
    for q in range(n_pos // 2):
        ls = slice(LANES * q, LANES * (q + 1))
        gb = jnp.where(low, gbs[2 * q], pltpu.roll(gbs[2 * q + 1], n_utt, 1))
        gl = jnp.where(low, gls[2 * q], pltpu.roll(gls[2 * q + 1], n_utt, 1))
        gb_r[:, ls] = gb
        gl_r[:, ls] = gl
        sc_r[:, ls] = (gb + gl) * rs_r[:, ls]

    u_rows = un.shape[1]
    h_rows = u_rows // 2
    p_rows = h_rows // nchip
    s_rows = p_rows // 2
    mine = core * h_rows

    def msg(kind, i, src, dst, dev):
        return pltpu.make_async_remote_copy(
            src_ref=src, dst_ref=dst, send_sem=snd.at[kind, i], recv_sem=rcv.at[kind, i],
            device_id={"seq": dev}, device_id_type=MESH)

    sent = []

    def send(*args):
        m = msg(*args)
        m.start()
        sent.append(m)

    def take(kind, i, ref):
        msg(kind, i, ref, ref, sib).wait_recv()

    def hp(i, k, lo, size):
        return un.at[i, pl.ds(mine + k * p_rows + lo, size)]

    narrow = (6, 7)

    def final(i, lo, size):
        return (gd.at[i - 6] if i in narrow else gg.at[i]).at[pl.ds(lo, size)]

    def gp(i, k, lo, size):
        return final(i, mine + k * p_rows + lo, size)

    def step0(i):
        send(M_D, i, un.at[i, pl.ds((1 - core) * h_rows, h_rows)], recvd.at[i], sib)

    def step1(i):
        take(M_D, i, recvd.at[i])
        un[i, pl.ds(mine, h_rows)] += recvd[i]
        send(M_R1L, i, hp(i, k_o, 0, s_rows), r1.at[i, 0], right)
        send(M_R1R, i, hp(i, k_o, s_rows, s_rows), r1.at[i, 1], left)
        send(M_DL, i, hp(i, k_r, s_rows, s_rows), dd.at[i, 0], right)
        send(M_DR, i, hp(i, k_l, 0, s_rows), dd.at[i, 1], left)

    def step2(i):
        take(M_R1L, i, r1.at[i, 0])
        t2[i, 0] = hp(i, k_r, 0, s_rows)[...] + r1[i, 0]
        send(M_R2L, i, t2.at[i, 0], r2.at[i, 0], right)
        take(M_R1R, i, r1.at[i, 1])
        t2[i, 1] = hp(i, k_l, s_rows, s_rows)[...] + r1[i, 1]
        send(M_R2R, i, t2.at[i, 1], r2.at[i, 1], left)

    def step3(i):
        take(M_DR, i, dd.at[i, 1])
        take(M_R2L, i, r2.at[i, 0])
        res, lo = (gd, i - 6) if i in narrow else (gg, i)
        res[lo, pl.ds(mine + chip * p_rows, s_rows)] = (hp(i, chip, 0, s_rows)[...] + r2[i, 0] + dd[i, 1]).astype(res.dtype)
        take(M_DL, i, dd.at[i, 0])
        take(M_R2R, i, r2.at[i, 1])
        res[lo, pl.ds(mine + chip * p_rows + s_rows, s_rows)] = (hp(i, chip, s_rows, s_rows)[...] + r2[i, 1] + dd[i, 0]).astype(res.dtype)
        own = gp(i, chip, 0, p_rows)
        send(M_AL, i, own, own, right)
        send(M_AR, i, own, own, left)

    def step4(i):
        take(M_AL, i, gp(i, k_l, 0, p_rows))
        send(M_OA, i, gp(i, k_l, 0, s_rows), gp(i, k_l, 0, s_rows), right)
        take(M_AR, i, gp(i, k_r, 0, p_rows))
        send(M_OB, i, gp(i, k_r, s_rows, s_rows), gp(i, k_r, s_rows, s_rows), left)

    def step5(i):
        take(M_OA, i, gp(i, k_o, 0, s_rows))
        take(M_OB, i, gp(i, k_o, s_rows, s_rows))
        half = final(i, mine, h_rows)
        send(M_S, i, half, half, sib)

    def step6(i):
        take(M_S, i, final(i, (1 - core) * h_rows, h_rows))

    steps = (step0, step1, step2, step3, step4, step5, step6)
    done = [0] * 8

    def advance(*units):
        for i in units:
            steps[done[i]](i)
            done[i] += 1

    vb = u_rows // hid * LANES
    dzs = (dz0, dz1, dz2, dz3)
    kc = n_row // 4

    dc = 32

    def dz_t(i, t):
        off = pl.multiple_of(t * rows_t, rows_t)
        cols = pl.ds(off, rows_t)
        sc = sc_r[pl.ds(t, 1), :]
        gl = gl_r[pl.ds(t, 1), :]
        row = iota((dc, rows_t), 0)
        for j in range(vb // dc):
            r0 = i * vb + dc * j
            x = e_s[r0:r0 + dc, cols] * sc
            x = jnp.where(row == lab_s[0:1, :] - r0, x - gl, x)
            if r0 == 0:
                x = jnp.where(row == 0, x - gb_r[pl.ds(t, 1), :], x)
            dzs[i][dc * j:dc * (j + 1), cols] = x.astype(BF16)

    def first_dz():
        def body(t, carry):
            dz_t(0, t)
            return carry
        lax.fori_loop(0, n_loc, body, 0)

    def out_part(i, part):
        def body(r, carry):
            lo = pl.multiple_of(r * kc, kc)
            x = mm(ht[:, pl.ds(lo, kc)], dzs[i][:, pl.ds(lo, kc)], NT)
            for s in range(2):
                y = x[:, s * LANES:(s + 1) * LANES]
                if part == 0:
                    y = y + jnp.where(r == 0, 0.0, un[i, s * hid:(s + 1) * hid])
                else:
                    y = y + un[i, s * hid:(s + 1) * hid]
                un[i, s * hid:(s + 1) * hid] = y
            if i < 3:
                dz_t(i + 1, 2 * r)
                dz_t(i + 1, 2 * r + 1)
            return carry
        lax.fori_loop(2 * part, 2 * part + 2, body, 0)

    def dh(blk, z_ref):
        cols = pl.ds(pl.multiple_of(blk * fb, fb), fb)
        x = mm(wo_ref[:, 0:vb], dz0[:, cols])
        for i in range(1, 4):
            x = x + mm(wo_ref[:, i * vb:(i + 1) * vb], dzs[i][:, cols])
        z_ref[0:hid, :] = x

    dr = 64

    def dp(t, half, z_ref):
        cols = pl.ds(pl.multiple_of(t * rows_t + half * fb, fb), fb)
        low = iota((dr, LANES), 1) < n_utt
        for i in range(hid // dr):
            rr = slice(dr * i, dr * (i + 1))
            h = ht[rr, cols].astype(F32)
            x = (z_ref[rr, :] * (1.0 - h * h)).astype(BF16).astype(F32)
            x0, x1 = x[:, 0:LANES], x[:, LANES:2 * LANES]
            un[6 + half, rr, :] += x0
            un[6 + half, hid + dr * i:hid + dr * (i + 1), :] += x1
            if half == 0:
                dacc[rr, :] = x0 + x1
            else:
                acc = x0 + x1 + dacc[rr, :]
                acc = acc + pltpu.roll(acc, n_utt, 1)
                dad[rr, pl.ds(pl.multiple_of(t * LANES, LANES), LANES)] = jnp.where(low, acc, 0.0).astype(BF16)

    n_back = 4

    def back(part):
        if part == 0:
            un[6:8] = jnp.zeros((2, u_rows, LANES), F32)
            dh(0, za)

        def body(t, carry):
            dh(2 * t + 1, zc)
            dp(t, 0, za)
            dh(jnp.minimum(2 * t + 2, n_blk - 1), za)
            dp(t, 1, zc)
            return carry

        lax.fori_loop(part * n_loc // n_back, (part + 1) * n_loc // n_back, body, 0)

    def grad_w_enc():
        da = mm(pd[...], dad[...], NT).astype(BF16)
        gf_ref[...] = mm(da, we_ref[...], NT).astype(BF16)
        x = mm(f_ref[...].T, da)
        for s in range(hid // LANES):
            lo, hi = s * enc, (s + 1) * enc
            first = lo
            while first < hi:
                unit = first // u_rows
                last = min(hi, (unit + 1) * u_rows)
                un[4 + unit, first - unit * u_rows:last - unit * u_rows] = x[first - lo:last - lo, s * LANES:(s + 1) * LANES]
                first = last

    segs = [(1.5, first_dz, ())]
    for i in range(4):
        for part in range(2):
            segs.append((.85, functools.partial(out_part, i, part), (i,) if part == 1 else ()))
    for part in range(n_back):
        segs.append((2.0, functools.partial(back, part), (6, 7) if part == n_back - 1 else ()))
    segs.append((2.0, grad_w_enc, (4, 5)))
    for what, i in static_order(segs, p_rows * LANES * 4, narrow):
        if what:
            advance(i)
        else:
            segs[i][1]()
    for m in sent:
        m.wait_send()
    for d in range(1, n):
        lat_copy(d, True).wait_send()


def finish(n_utt, enc, loss_in, gf_in, gg, gd, gpt, loss_ref, gf_ref, gwe_ref, gwp_ref, gwo_ref, sem):
    hid = gpt.shape[0]
    u_rows = gg.shape[1]
    copies = []

    def copy(src, dst):
        cp = pltpu.make_async_copy(src, dst, sem.at[len(copies)])
        cp.start()
        copies.append(cp)

    for i in range(4):
        for s in range(2):
            lo = (2 * i + s) * LANES
            copy(gg.at[i, pl.ds(s * hid, hid)], gwo_ref.at[:, pl.ds(lo, LANES)])
    copy(gf_in, gf_ref)
    for s in range(hid // LANES):
        lo, hi = s * enc, (s + 1) * enc
        first = lo
        while first < hi:
            unit = first // u_rows
            last = min(hi, (unit + 1) * u_rows)
            copy(gg.at[4 + unit, pl.ds(first - unit * u_rows, last - first)],
                 gwe_ref.at[pl.ds(first - lo, last - first), pl.ds(s * LANES, LANES)])
            first = last
    loss_ref[...] = loss_in[0:1, 0:n_utt].reshape(n_utt)
    dcb = jnp.concatenate([gd[0, 0:hid], gd[0, hid:2 * hid], gd[1, 0:hid], gd[1, hid:2 * hid]], axis=1)
    gwp_ref[...] = mm(gpt[...], dcb, NT)
    for cp in copies:
        cp.wait()


def solution(mesh):
    n = mesh.shape["seq"]

    def local_fn(enc_out, pred_out, w_enc, w_pred, w_out, labels, frame_len, label_len):
        n_utt, n_loc, enc = enc_out.shape
        n_pos, pred = pred_out.shape[1:]
        hid, voc = w_out.shape
        assert n == 8 and 2 * n_utt == LANES and n_loc == 8 and n_pos == 8
        n_bt = n_utt * n_loc
        rows_t = n_utt * n_pos
        n_row = n_loc * rows_t
        u_rows = 2 * hid
        h_rows = u_rows // 2
        s_rows = h_rows // n
        vm = pl.BlockSpec(memory_space=pltpu.VMEM)
        anys = pl.BlockSpec(memory_space=pl.ANY)
        n_sk = (n * n_loc + n_pos) * n_pos
        vmem = pltpu.VMEM
        scratch = [
            vmem((voc, hid), BF16),
            vmem((hid, n_loc * LANES), BF16),
            vmem((hid, rows_t), BF16),
            vmem((hid, n_row), BF16),
            vmem((voc, n_row), F32),
            vmem((voc, rows_t // 2), F32),
            vmem((voc, rows_t // 2), F32),
        ] + [vmem((voc // 4, n_row), BF16)] * 4 + [
            vmem((hid, n_loc * LANES), BF16),
            vmem((hid, LANES), F32),
            vmem((n_bt, n_loc * LANES), BF16),
            vmem((n_pos, LANES), jnp.int32),
            vmem((8, rows_t), jnp.int32),
            vmem((8, LANES), jnp.int32),
        ] + [vmem((n_loc, rows_t), F32)] * 6 + [
            vmem((n_loc * n_pos, LANES), F32),
            vmem((n, n_loc * n_pos, LANES), F32),
        ] + [vmem((n_sk, LANES), F32)] * 5 + [
            vmem((8, u_rows, LANES), F32),
            vmem((8, h_rows, LANES), F32),
        ] + [vmem((8, 2, s_rows, LANES), F32)] * 4 + [
            pltpu.SemaphoreType.DMA((n,)),
            pltpu.SemaphoreType.DMA((n,)),
            pltpu.SemaphoreType.DMA((12, 8)),
            pltpu.SemaphoreType.DMA((12, 8)),
        ]
        mid = pl.pallas_call(
            functools.partial(kernel, n, n_utt, n_loc, n_pos),
            out_shape=(
                vmem((8, LANES), F32),
                vmem((n_bt, enc), BF16),
                vmem((6, u_rows, LANES), F32),
                vmem((2, u_rows, LANES), BF16),
                vmem((hid, rows_t), BF16),
            ),
            in_specs=[vm] * 8,
            out_specs=(vm,) * 5,
            scratch_shapes=scratch,
            compiler_params=pltpu.CompilerParams(collective_id=0, has_side_effects=True, vmem_limit_bytes=VMEM_LIMIT),
            name="rnnt",
        )(enc_out.reshape(n_bt, enc), pred_out.reshape(n_utt * n_pos, pred), w_enc, w_pred, w_out, labels.T, frame_len.reshape(1, n_utt), label_len.reshape(1, n_utt))
        mid = [pltpu.with_memory_space_constraint(x, pltpu.VMEM) for x in mid]
        loss, gf, gwe, gwp, gwo = pl.pallas_call(
            functools.partial(finish, n_utt, enc),
            out_shape=(
                jax.ShapeDtypeStruct((n_utt,), F32),
                jax.ShapeDtypeStruct((n_bt, enc), BF16),
                jax.ShapeDtypeStruct((enc, hid), F32),
                jax.ShapeDtypeStruct((pred, hid), F32),
                jax.ShapeDtypeStruct((hid, voc), F32),
            ),
            in_specs=[vm] * 5,
            out_specs=(vm, anys, anys, vm, anys),
            scratch_shapes=[pltpu.SemaphoreType.DMA((24,))],
            compiler_params=pltpu.CompilerParams(vmem_limit_bytes=8 * 2 ** 20),
            name="finish",
        )(*mid)
        return loss, gf.reshape(n_utt, n_loc, enc), gwe, gwp, gwo

    in_specs = (P("dp", "seq", None), P("dp", None, None), P(None, None), P(None, None), P(None, None), P("dp", None), P("dp"), P("dp"))
    out_specs = (P("dp"), P("dp", "seq", None), P("dp", None), P("dp", None), P("dp", None))
    return jax.shard_map(local_fn, mesh=mesh, in_specs=in_specs, out_specs=out_specs, check_vma=False)
```

time: 112 us -> 87.2 us (0.78)
  Pallas kernels: 99.7 us -> 86.3 us
  local copies, waits for them, and re-layouts: 10.3 us -> 0 us
  other arithmetic: 1.41 us -> 0 us
    pallas_call x1, Pallas kernels: 99.7 us -> 82.5 us  [local_fn(): pl.pallas_call(functools.partial(kernel, n, n_utt, n_loc, n_pos), out_sha...]
    unnamed x8 -> x0, local copies, waits for them, and re-layouts: 8.27 us -> none
    pallas_call x0 -> x1, Pallas kernels: none -> 3.79 us  [local_fn(): pl.pallas_call(functools.partial(finish, n_utt, enc), out_shape=(jax.Shap...]
    concatenate x1 -> x0, other arithmetic: 1.41 us -> none  [local_fn(): jnp.concatenate([lab, lens, jnp.zeros((2, LANES), jnp.int32)], axis=0)]
    squeeze x1 -> x0, local copies, waits for them, and re-layouts: 1.18 us -> none  [local_fn(): return (loss[0, :n_utt], gf.reshape(n_utt, n_loc, enc), gwe, gwp, gwo)]
where the time goes in v2:
time: 87.2 us; the launch traced here: 87.1 us
  Pallas kernels  86.3 us (99%)
    pallas_call x1, Pallas kernels, local_fn(): pl.pallas_call(functools.partial(kernel, n, n_utt, n_loc, n_pos), out_sha...  82.5 us
    pallas_call x1, Pallas kernels, local_fn(): pl.pallas_call(functools.partial(finish, n_utt, enc), out_shape=(jax.Shap...  3.79 us

profile of v2, /device:TPU:113, one launch (start us, length us, event | category | flops | bytes accessed | tf_op | source)
XLA Modules:
  0.0 87.1 jit_solution(4523073499992466167)
XLA Ops:
  0.6 82.5 %rnnt.1 = (f32[8,128]{1,0:T(8,128)S(1)}, bf16[512,512]{1,0:T(8,128)(2,1)S(1)}, f32[6,1280,128]{2,1,0:T(8,128)S(1)}, bf16[2,1280,128]{2,1,0:T(8,128)(2,1)S(1)}, bf16[640,512]{1,0:T(8,128)(2,1)S(1)}) custom-call(bf16[512,512]{1,0:T(8,128)(2,1)} %bitcast.7, bf16[512,640]{1,0:T(8,128)(2,1)} %bitcast.6, bf16[512,640]{1,0:T(8,128)(2,1)} %we_ref.1, ...), custom_call_target="tpu_custom_call" | custom-call | tf_op jit(solution)/shard_map/rnnt/pallas_call | solution.py:551
  83.2 3.8 %finish.1 = (f32[64]{0:T(128)}, bf16[512,512]{1,0:T(8,128)(2,1)}, f32[512,640]{1,0:T(8,128)}, f32[640,640]{1,0:T(8,128)}, f32[640,1024]{1,0:T(8,128)}) custom-call(f32[8,128]{1,0:T(8,128)S(1)} %get-tuple-element.15.loss_in, bf16[512,512]{1,0:T(8,128)(2,1)S(1)} %get-tuple-element.16.gf_in, f32[6,1280,128]{2,1,0:T(8,128)S(1)} %get-tuple-element.17.gg, ...), custom_call_target="tpu_custom_call" | custom-call | tf_op jit(solution)/shard_map/finish/pallas_call | solution.py:567

commit v3 on v2

--- a/solution.py
+++ b/solution.py
@@ -12,10 +12,11 @@
 BF16 = jnp.bfloat16
 MESH = pl.DeviceIdType.MESH
 LANES = 128
+N_BACK = 8
 VMEM_LIMIT = 57 * 2 ** 20
 NT = (((1,), (1,)), ((), ()))
 NN = (((1,), (0,)), ((), ()))
-M_D, M_R1L, M_R1R, M_DL, M_DR, M_R2L, M_R2R, M_AL, M_AR, M_OA, M_OB, M_S = range(12)
+M_D, M_R1L, M_R1R, M_DL, M_DR, M_R2L, M_R2R, M_AL, M_AR, M_OA, M_OB, M_SC, M_SL, M_SR, M_SO = range(15)
 
 
 def mm(a, b, dims=NN):
@@ -30,8 +31,8 @@
     return jnp.maximum(x, y) + jnp.log(1.0 + jnp.exp(-jnp.abs(x - y)))
 
 
-LINK_RATE, LINK_LAT, CORE_RATE, CORE_LAT = 46.6e3, 1.9, 600e3, 1.1
-NEEDS = ((), (M_D,), (M_R1L, M_R1R), (M_DL, M_DR, M_R2L, M_R2R), (M_AL, M_AR), (M_OA, M_OB), (M_S,))
+LINK_RATE, LINK_LAT, CORE_RATE, CORE_LAT = 46.6e3, 2.5, 600e3, 1.4
+NEEDS = ((), (M_D,), (M_R1L, M_R1R), (M_DL, M_DR, M_R2L, M_R2R), (M_AL, M_AR), (M_OA, M_OB), (M_SC, M_SL, M_SR, M_SO))
 COSTS = (.02, .25, .1, .2, .05, .05, .05)
 
 
@@ -63,11 +64,14 @@
         elif k == 3:
             tx(M_AL, u, "r", ag)
             tx(M_AR, u, "l", ag)
+            tx(M_SC, u, "c", ag)
         elif k == 4:
             tx(M_OA, u, "r", ag / 2)
             tx(M_OB, u, "l", ag / 2)
+            tx(M_SL, u, "c", ag)
+            tx(M_SR, u, "c", ag)
         elif k == 5:
-            tx(M_S, u, "c", 4 * ag)
+            tx(M_SO, u, "c", ag)
         done[u] += 1
         order.append((1, u))
 
@@ -91,13 +95,19 @@
 
 
 def kernel(n, n_utt, n_loc, n_pos,
-           f_ref, g_ref, we_ref, wp_ref, wo_ref, lab_ref, flen_ref, llen_ref,
+           f_in, g_in, we_in, wp_in, wo_in, lab_in, flen_in, llen_in,
            loss_ref, gf_ref, gg, gd, gpt_ref,
-           wot, at_s, ct_s, ht, e_s, za, zc, dz0, dz1, dz2, dz3, dad, dacc, pd, trs, lab_s, len_s,
+           wot, at_s, ct_s, ht, e_s, za, zc, dz0, dz1, dz2, dz3, dad, das, dacc, pd, trs, lab_s, len_s,
            blank_r, lab_r, rs_r, gb_r, gl_r, sc_r,
            pm, recvp, sp, sr, sa, xb, yb,
            un, recvd, r1, dd, r2, t2,
-           lat_s, lat_r, snd, rcv):
+           f_ref, g_ref, we_ref, wp_ref, wo_ref, lab_ref, flen_ref, llen_ref,
+           lat_s, lat_r, snd, rcv, in_sem):
+    loads = [pltpu.make_async_copy(src, dst, in_sem.at[q]) for q, (src, dst) in enumerate((
+        (we_in, we_ref), (f_in, f_ref), (wp_in, wp_ref), (g_in, g_ref), (wo_in, wo_ref),
+        (lab_in, lab_ref), (flen_in, flen_ref), (llen_in, llen_ref)))]
+    for cp in loads:
+        cp.start()
     me = lax.axis_index("seq")
     nchip = n // 2
     chip, core = me // 2, lax.rem(me, 2)
@@ -114,6 +124,21 @@
     for d in range(1, n):
         pl.semaphore_signal(barrier, inc=1, device_id={"seq": lax.rem(me + d, n)}, device_id_type=MESH)
 
+    key_r = lax.rem(iota((n_bt, 1), 0), n_loc) * n_utt + iota((n_bt, 1), 0) // n_loc
+    col = iota((1, 2 * n_bt), 1)
+    key_c = (col // LANES) * n_utt + lax.rem(col, n_utt)
+    pd[...] = jnp.where(key_r == key_c, 1.0, 0.0).astype(BF16)
+    pc = jnp.where(key_r == iota((1, rows_t), 1), 1.0, 0.0).astype(BF16)
+    loads[0].wait()
+    loads[1].wait()
+    at = mm(we_ref[...].T, f_ref[...], NT).astype(BF16)
+    at_s[...] = mm(at, pd[...]).astype(BF16)
+    loads[2].wait()
+    loads[3].wait()
+    ct = mm(wp_ref[...].T, g_ref[...], NT).astype(BF16)
+    ct_s[...] = mm(ct, pc).astype(BF16)
+    for cp in loads[4:]:
+        cp.wait()
     wot[...] = wo_ref[...].T
     trs[...] = jnp.full(trs.shape, -1, jnp.int32)
     trs[0:n_pos - 1, 0:n_utt] = lab_ref[...]
@@ -124,16 +149,6 @@
         lab_s[0:1, LANES * q:LANES * (q + 1)] = jnp.where(low1, lab_t[2 * q:2 * q + 1], lab_alt[2 * q + 1:2 * q + 2])
     len_s[0:1, 0:n_utt] = flen_ref[...]
     len_s[1:2, 0:n_utt] = llen_ref[...]
-    key_r = lax.rem(iota((n_bt, 1), 0), n_loc) * n_utt + iota((n_bt, 1), 0) // n_loc
-    col = iota((1, 2 * n_bt), 1)
-    key_c = (col // LANES) * n_utt + lax.rem(col, n_utt)
-    pd[...] = jnp.where(key_r == key_c, 1.0, 0.0).astype(BF16)
-    pc = jnp.where(key_r == iota((1, rows_t), 1), 1.0, 0.0).astype(BF16)
-    at = mm(we_ref[...].T, f_ref[...], NT).astype(BF16)
-    at_s[...] = mm(at, pd[...]).astype(BF16)
-    ct = mm(wp_ref[...].T, g_ref[...], NT).astype(BF16)
-    ct_s[...] = mm(ct, pc).astype(BF16)
-    gpt_ref[...] = mm(g_ref[...].T, pc).astype(BF16)
 
     fb = rows_t // 2
     n_blk = n_row // fb
@@ -207,14 +222,18 @@
 
     pl.semaphore_wait(barrier, n - 1)
 
-    def lat_copy(d, dst):
-        peer = lax.rem(me + d, n)
+    opp = k_o * 2 + core
+    opp_x = k_o * 2 + 1 - core
+
+    def lat_copy(q, src, slot, dev):
         return pltpu.make_async_remote_copy(
-            src_ref=pm, dst_ref=recvp.at[me if dst else peer], send_sem=lat_s.at[d],
-            recv_sem=lat_r.at[me if dst else peer], device_id={"seq": peer}, device_id_type=MESH)
-
-    for d in range(1, n):
-        lat_copy(d, True).start()
+            src_ref=src, dst_ref=recvp.at[slot], send_sem=lat_s.at[q], recv_sem=lat_r.at[slot],
+            device_id={"seq": dev}, device_id_type=MESH)
+
+    lat_sent = [lat_copy(q, pm, me, dev) for q, dev in enumerate(
+        (opp, right, left, k_r * 2 + 1 - core, k_l * 2 + 1 - core, sib))]
+    for m in lat_sent:
+        m.start()
 
     fill_lane = iota(sp.shape, 1) < n_utt
     sp[...] = jnp.where(fill_lane, 0.0, NEG)
@@ -231,10 +250,13 @@
             sr[pl.ds(base, n_loc, stride=n_pos), :] = pltpu.roll(x, n_utt, 1)
 
     put(me * (n_loc * n_pos), pm)
-    for d in range(1, n):
-        peer = lax.rem(me + d, n)
-        lat_copy(d, False).wait_recv()
-        put(peer * (n_loc * n_pos), recvp.at[peer])
+    for slot in (sib, right, left, k_r * 2 + 1 - core, k_l * 2 + 1 - core, opp, opp_x):
+        lat_copy(0, pm, slot, sib).wait_recv()
+        if slot is opp:
+            relay = lat_copy(6, recvp.at[opp], opp, sib)
+            relay.start()
+            lat_sent.append(relay)
+        put(slot * (n_loc * n_pos), recvp.at[slot])
 
     n_diag = n * n_loc + n_pos - 1
 
@@ -332,21 +354,24 @@
         own = gp(i, chip, 0, p_rows)
         send(M_AL, i, own, own, right)
         send(M_AR, i, own, own, left)
+        send(M_SC, i, own, own, sib)
 
     def step4(i):
         take(M_AL, i, gp(i, k_l, 0, p_rows))
         send(M_OA, i, gp(i, k_l, 0, s_rows), gp(i, k_l, 0, s_rows), right)
         take(M_AR, i, gp(i, k_r, 0, p_rows))
         send(M_OB, i, gp(i, k_r, s_rows, s_rows), gp(i, k_r, s_rows, s_rows), left)
+        send(M_SL, i, gp(i, k_l, 0, p_rows), gp(i, k_l, 0, p_rows), sib)
+        send(M_SR, i, gp(i, k_r, 0, p_rows), gp(i, k_r, 0, p_rows), sib)
 
     def step5(i):
         take(M_OA, i, gp(i, k_o, 0, s_rows))
         take(M_OB, i, gp(i, k_o, s_rows, s_rows))
-        half = final(i, mine, h_rows)
-        send(M_S, i, half, half, sib)
+        send(M_SO, i, gp(i, k_o, 0, p_rows), gp(i, k_o, 0, p_rows), sib)
 
     def step6(i):
-        take(M_S, i, final(i, (1 - core) * h_rows, h_rows))
+        for kind, k in ((M_SC, chip), (M_SL, k_l), (M_SR, k_r), (M_SO, k_o)):
+            take(kind, i, final(i, (1 - core) * h_rows + k * p_rows, p_rows))
 
     steps = (step0, step1, step2, step3, step4, step5, step6)
     done = [0] * 8
@@ -376,9 +401,9 @@
                 x = jnp.where(row == 0, x - gb_r[pl.ds(t, 1), :], x)
             dzs[i][dc * j:dc * (j + 1), cols] = x.astype(BF16)
 
-    def first_dz():
+    def all_dz(i):
         def body(t, carry):
-            dz_t(0, t)
+            dz_t(i, t)
             return carry
         lax.fori_loop(0, n_loc, body, 0)
 
@@ -393,9 +418,6 @@
                 else:
                     y = y + un[i, s * hid:(s + 1) * hid]
                 un[i, s * hid:(s + 1) * hid] = y
-            if i < 3:
-                dz_t(i + 1, 2 * r)
-                dz_t(i + 1, 2 * r + 1)
             return carry
         lax.fori_loop(2 * part, 2 * part + 2, body, 0)
 
@@ -425,7 +447,7 @@
                 acc = acc + pltpu.roll(acc, n_utt, 1)
                 dad[rr, pl.ds(pl.multiple_of(t * LANES, LANES), LANES)] = jnp.where(low, acc, 0.0).astype(BF16)
 
-    n_back = 4
+    n_back = N_BACK
 
     def back(part):
         if part == 0:
@@ -441,9 +463,13 @@
 
         lax.fori_loop(part * n_loc // n_back, (part + 1) * n_loc // n_back, body, 0)
 
+    def pred_t():
+        pc2 = jnp.where(key_r == iota((1, rows_t), 1), 1.0, 0.0).astype(BF16)
+        gpt_ref[...] = mm(g_ref[...].T, pc2).astype(BF16)
+
     def grad_w_enc():
         da = mm(pd[...], dad[...], NT).astype(BF16)
-        gf_ref[...] = mm(da, we_ref[...], NT).astype(BF16)
+        das[...] = da
         x = mm(f_ref[...].T, da)
         for s in range(hid // LANES):
             lo, hi = s * enc, (s + 1) * enc
@@ -454,13 +480,19 @@
                 un[4 + unit, first - unit * u_rows:last - unit * u_rows] = x[first - lo:last - lo, s * LANES:(s + 1) * LANES]
                 first = last
 
-    segs = [(1.5, first_dz, ())]
+    def grad_enc():
+        gf_ref[...] = mm(das[...], we_ref[...], NT).astype(BF16)
+
+    segs = []
     for i in range(4):
+        segs.append((.9, functools.partial(all_dz, i), ()))
         for part in range(2):
-            segs.append((.85, functools.partial(out_part, i, part), (i,) if part == 1 else ()))
+            segs.append((1.3, functools.partial(out_part, i, part), (i,) if part == 1 else ()))
     for part in range(n_back):
-        segs.append((2.0, functools.partial(back, part), (6, 7) if part == n_back - 1 else ()))
-    segs.append((2.0, grad_w_enc, (4, 5)))
+        segs.append((9.2 / n_back, functools.partial(back, part), (6, 7) if part == n_back - 1 else ()))
+    segs.append((1.8, grad_w_enc, (4, 5)))
+    segs.append((.6, grad_enc, ()))
+    segs.append((.6, pred_t, ()))
     for what, i in static_order(segs, p_rows * LANES * 4, narrow):
         if what:
             advance(i)
@@ -468,11 +500,11 @@
             segs[i][1]()
     for m in sent:
         m.wait_send()
-    for d in range(1, n):
-        lat_copy(d, True).wait_send()
-
-
-def finish(n_utt, enc, loss_in, gf_in, gg, gd, gpt, loss_ref, gf_ref, gwe_ref, gwp_ref, gwo_ref, sem):
+    for m in lat_sent:
+        m.wait_send()
+
+
+def finish(n_utt, enc, loss_in, gf_in, gg, gd, gpt, loss_ref, gf_ref, gwe_ref, gwp_ref, gwo_ref, gwp_s, sem):
     hid = gpt.shape[0]
     u_rows = gg.shape[1]
     copies = []
@@ -498,7 +530,10 @@
             first = last
     loss_ref[...] = loss_in[0:1, 0:n_utt].reshape(n_utt)
     dcb = jnp.concatenate([gd[0, 0:hid], gd[0, hid:2 * hid], gd[1, 0:hid], gd[1, hid:2 * hid]], axis=1)
-    gwp_ref[...] = mm(gpt[...], dcb, NT)
+    for lo in range(0, hid, 2 * LANES):
+        size = min(2 * LANES, hid - lo)
+        gwp_s[:, lo:lo + size] = mm(gpt[...], dcb[lo:lo + size], NT)
+        copy(gwp_s.at[:, pl.ds(lo, size)], gwp_ref.at[:, pl.ds(lo, size)])
     for cp in copies:
         cp.wait()
 
@@ -531,6 +566,7 @@
             vmem((voc, rows_t // 2), F32),
         ] + [vmem((voc // 4, n_row), BF16)] * 4 + [
             vmem((hid, n_loc * LANES), BF16),
+            vmem((n_bt, hid), BF16),
             vmem((hid, LANES), F32),
             vmem((n_bt, n_loc * LANES), BF16),
             vmem((n_pos, LANES), jnp.int32),
@@ -543,10 +579,19 @@
             vmem((8, u_rows, LANES), F32),
             vmem((8, h_rows, LANES), F32),
         ] + [vmem((8, 2, s_rows, LANES), F32)] * 4 + [
+            vmem((n_bt, enc), BF16),
+            vmem((n_utt * n_pos, pred), BF16),
+            vmem((enc, hid), BF16),
+            vmem((pred, hid), BF16),
+            vmem((hid, voc), BF16),
+            vmem((n_pos - 1, n_utt), jnp.int32),
+            vmem((1, n_utt), jnp.int32),
+            vmem((1, n_utt), jnp.int32),
             pltpu.SemaphoreType.DMA((n,)),
             pltpu.SemaphoreType.DMA((n,)),
-            pltpu.SemaphoreType.DMA((12, 8)),
-            pltpu.SemaphoreType.DMA((12, 8)),
+            pltpu.SemaphoreType.DMA((15, 8)),
+            pltpu.SemaphoreType.DMA((15, 8)),
+            pltpu.SemaphoreType.DMA((8,)),
         ]
         mid = pl.pallas_call(
             functools.partial(kernel, n, n_utt, n_loc, n_pos),
@@ -557,7 +602,7 @@
                 vmem((2, u_rows, LANES), BF16),
                 vmem((hid, rows_t), BF16),
             ),
-            in_specs=[vm] * 8,
+            in_specs=[pl.BlockSpec(memory_space=pltpu.HBM)] * 8,
             out_specs=(vm,) * 5,
             scratch_shapes=scratch,
             compiler_params=pltpu.CompilerParams(collective_id=0, has_side_effects=True, vmem_limit_bytes=VMEM_LIMIT),
@@ -574,8 +619,8 @@
                 jax.ShapeDtypeStruct((hid, voc), F32),
             ),
             in_specs=[vm] * 5,
-            out_specs=(vm, anys, anys, vm, anys),
-            scratch_shapes=[pltpu.SemaphoreType.DMA((24,))],
+            out_specs=(vm, anys, anys, anys, anys),
+            scratch_shapes=[vmem((pred, hid), F32), pltpu.SemaphoreType.DMA((24,))],
             compiler_params=pltpu.CompilerParams(vmem_limit_bytes=8 * 2 ** 20),
             name="finish",
         )(*mid)

time: 87.2 us -> 86.2 us (0.989)
  Pallas kernels: 86.3 us -> 85.3 us
where the time goes in v3:
time: 86.2 us; the launch traced here: 86.1 us
  Pallas kernels  85.3 us (99%)
    pallas_call x1, Pallas kernels, local_fn(): pl.pallas_call(functools.partial(kernel, n, n_utt, n_loc, n_pos), out_sha...  81.9 us
    pallas_call x1, Pallas kernels, local_fn(): pl.pallas_call(functools.partial(finish, n_utt, enc), out_shape=(jax.Shap...  3.47 us

profile of v3, /device:TPU:113, one launch (start us, length us, event | category | flops | bytes accessed | tf_op | source)
XLA Modules:
  0.0 86.1 jit_solution(7256300444881434895)
XLA Ops:
  0.6 81.9 %rnnt.1 = (f32[8,128]{1,0:T(8,128)S(1)}, bf16[512,512]{1,0:T(8,128)(2,1)S(1)}, f32[6,1280,128]{2,1,0:T(8,128)S(1)}, bf16[2,1280,128]{2,1,0:T(8,128)(2,1)S(1)}, bf16[640,512]{1,0:T(8,128)(2,1)S(1)}) custom-call(bf16[512,512]{1,0:T(8,128)(2,1)} %bitcast.7, bf16[512,640]{1,0:T(8,128)(2,1)} %bitcast.6, bf16[512,640]{1,0:T(8,128)(2,1)} %we_in.1, ...), custom_call_target="tpu_custom_call" | custom-call | tf_op jit(solution)/shard_map/rnnt/pallas_call | solution.py:596
  82.5 3.5 %finish.1 = (f32[64]{0:T(128)}, bf16[512,512]{1,0:T(8,128)(2,1)}, f32[512,640]{1,0:T(8,128)}, f32[640,640]{1,0:T(8,128)}, f32[640,1024]{1,0:T(8,128)}) custom-call(f32[8,128]{1,0:T(8,128)S(1)} %get-tuple-element.15.loss_in, bf16[512,512]{1,0:T(8,128)(2,1)S(1)} %get-tuple-element.16.gf_in, f32[6,1280,128]{2,1,0:T(8,128)S(1)} %get-tuple-element.17.gg, ...), custom_call_target="tpu_custom_call" | custom-call | tf_op jit(solution)/shard_map/finish/pallas_call | solution.py:612

commit v4 on v3

--- a/solution.py
+++ b/solution.py
@@ -96,8 +96,8 @@
 
 def kernel(n, n_utt, n_loc, n_pos,
            f_in, g_in, we_in, wp_in, wo_in, lab_in, flen_in, llen_in,
-           loss_ref, gf_ref, gg, gd, gpt_ref,
-           wot, at_s, ct_s, ht, e_s, za, zc, dz0, dz1, dz2, dz3, dad, das, dacc, pd, trs, lab_s, len_s,
+           loss_ref, gf_ref, gg, gwp_ref,
+           gd, wot, at_s, ct_s, ht, e_s, za, zc, dz0, dz1, dz2, dz3, dad, dacc, pd, trs, lab_s, len_s,
            blank_r, lab_r, rs_r, gb_r, gl_r, sc_r,
            pm, recvp, sp, sr, sa, xb, yb,
            un, recvd, r1, dd, r2, t2,
@@ -465,11 +465,11 @@
 
     def pred_t():
         pc2 = jnp.where(key_r == iota((1, rows_t), 1), 1.0, 0.0).astype(BF16)
-        gpt_ref[...] = mm(g_ref[...].T, pc2).astype(BF16)
+        ct_s[...] = mm(g_ref[...].T, pc2).astype(BF16)
 
     def grad_w_enc():
         da = mm(pd[...], dad[...], NT).astype(BF16)
-        das[...] = da
+        at_s[0:n_bt, 0:hid] = da
         x = mm(f_ref[...].T, da)
         for s in range(hid // LANES):
             lo, hi = s * enc, (s + 1) * enc
@@ -480,8 +480,12 @@
                 un[4 + unit, first - unit * u_rows:last - unit * u_rows] = x[first - lo:last - lo, s * LANES:(s + 1) * LANES]
                 first = last
 
+    def grad_w_pred():
+        dcb = jnp.concatenate([gd[0, 0:hid], gd[0, hid:2 * hid], gd[1, 0:hid], gd[1, hid:2 * hid]], axis=1)
+        gwp_ref[...] = mm(ct_s[...], dcb, NT)
+
     def grad_enc():
-        gf_ref[...] = mm(das[...], we_ref[...], NT).astype(BF16)
+        gf_ref[...] = mm(at_s[0:n_bt, 0:hid], we_ref[...], NT).astype(BF16)
 
     segs = []
     for i in range(4):
@@ -496,6 +500,8 @@
     for what, i in static_order(segs, p_rows * LANES * 4, narrow):
         if what:
             advance(i)
+            if i in narrow and done[6] == done[7] == 7:
+                grad_w_pred()
         else:
             segs[i][1]()
     for m in sent:
@@ -504,8 +510,8 @@
         m.wait_send()
 
 
-def finish(n_utt, enc, loss_in, gf_in, gg, gd, gpt, loss_ref, gf_ref, gwe_ref, gwp_ref, gwo_ref, gwp_s, sem):
-    hid = gpt.shape[0]
+def finish(n_utt, enc, loss_in, gf_in, gg, gwp_in, loss_ref, gf_ref, gwe_ref, gwp_ref, gwo_ref, sem):
+    hid = gwp_in.shape[1]
     u_rows = gg.shape[1]
     copies = []
 
@@ -519,6 +525,7 @@
             lo = (2 * i + s) * LANES
             copy(gg.at[i, pl.ds(s * hid, hid)], gwo_ref.at[:, pl.ds(lo, LANES)])
     copy(gf_in, gf_ref)
+    copy(gwp_in, gwp_ref)
     for s in range(hid // LANES):
         lo, hi = s * enc, (s + 1) * enc
         first = lo
@@ -529,11 +536,6 @@
                  gwe_ref.at[pl.ds(first - lo, last - first), pl.ds(s * LANES, LANES)])
             first = last
     loss_ref[...] = loss_in[0:1, 0:n_utt].reshape(n_utt)
-    dcb = jnp.concatenate([gd[0, 0:hid], gd[0, hid:2 * hid], gd[1, 0:hid], gd[1, hid:2 * hid]], axis=1)
-    for lo in range(0, hid, 2 * LANES):
-        size = min(2 * LANES, hid - lo)
-        gwp_s[:, lo:lo + size] = mm(gpt[...], dcb[lo:lo + size], NT)
-        copy(gwp_s.at[:, pl.ds(lo, size)], gwp_ref.at[:, pl.ds(lo, size)])
     for cp in copies:
         cp.wait()
 
@@ -557,6 +559,7 @@
         n_sk = (n * n_loc + n_pos) * n_pos
         vmem = pltpu.VMEM
         scratch = [
+            vmem((2, u_rows, LANES), BF16),
             vmem((voc, hid), BF16),
             vmem((hid, n_loc * LANES), BF16),
             vmem((hid, rows_t), BF16),
@@ -566,7 +569,6 @@
             vmem((voc, rows_t // 2), F32),
         ] + [vmem((voc // 4, n_row), BF16)] * 4 + [
             vmem((hid, n_loc * LANES), BF16),
-            vmem((n_bt, hid), BF16),
             vmem((hid, LANES), F32),
             vmem((n_bt, n_loc * LANES), BF16),
             vmem((n_pos, LANES), jnp.int32),
@@ -599,11 +601,10 @@
                 vmem((8, LANES), F32),
                 vmem((n_bt, enc), BF16),
                 vmem((6, u_rows, LANES), F32),
-                vmem((2, u_rows, LANES), BF16),
-                vmem((hid, rows_t), BF16),
+                vmem((pred, hid), F32),
             ),
             in_specs=[pl.BlockSpec(memory_space=pltpu.HBM)] * 8,
-            out_specs=(vm,) * 5,
+            out_specs=(vm,) * 4,
             scratch_shapes=scratch,
             compiler_params=pltpu.CompilerParams(collective_id=0, has_side_effects=True, vmem_limit_bytes=VMEM_LIMIT),
             name="rnnt",
@@ -618,10 +619,10 @@
                 jax.ShapeDtypeStruct((pred, hid), F32),
                 jax.ShapeDtypeStruct((hid, voc), F32),
             ),
-            in_specs=[vm] * 5,
+            in_specs=[vm] * 4,
             out_specs=(vm, anys, anys, anys, anys),
-            scratch_shapes=[vmem((pred, hid), F32), pltpu.SemaphoreType.DMA((24,))],
-            compiler_params=pltpu.CompilerParams(vmem_limit_bytes=8 * 2 ** 20),
+            scratch_shapes=[pltpu.SemaphoreType.DMA((24,))],
+            compiler_params=pltpu.CompilerParams(vmem_limit_bytes=2 ** 20),
             name="finish",
         )(*mid)
         return loss, gf.reshape(n_utt, n_loc, enc), gwe, gwp, gwo

time: 86.2 us -> 86.1 us (level)
  no operation moved by 1% of the time
where the time goes in v4:
time: 86.1 us
  Pallas kernels  85.2 us (99%)
    pallas_call x1, Pallas kernels, local_fn(): pl.pallas_call(functools.partial(kernel, n, n_utt, n_loc, n_pos), out_sha...  81.9 us
    pallas_call x1, Pallas kernels, local_fn(): pl.pallas_call(functools.partial(finish, n_utt, enc), out_shape=(jax.Shap...  3.31 us

profile of v4, /device:TPU:113, one launch (start us, length us, event | category | flops | bytes accessed | tf_op | source)
XLA Modules:
  0.0 86.1 jit_solution(13888372835261316047)
XLA Ops:
  0.6 81.9 %rnnt.1 = (f32[8,128]{1,0:T(8,128)S(1)}, bf16[512,512]{1,0:T(8,128)(2,1)S(1)}, f32[6,1280,128]{2,1,0:T(8,128)S(1)}, f32[640,640]{1,0:T(8,128)S(1)}) custom-call(bf16[512,512]{1,0:T(8,128)(2,1)} %bitcast.7, bf16[512,640]{1,0:T(8,128)(2,1)} %bitcast.6, bf16[512,640]{1,0:T(8,128)(2,1)} %we_in.1, bf16[640,640]{1,0:T(8,128)(2,1)} %wp_in.1, ...), custom_call_target="tpu_custom_call" | custom-call | tf_op jit(solution)/shard_map/rnnt/pallas_call | solution.py:598
  82.6 3.3 %finish.1 = (f32[64]{0:T(128)}, bf16[512,512]{1,0:T(8,128)(2,1)}, f32[512,640]{1,0:T(8,128)}, f32[640,640]{1,0:T(8,128)}, f32[640,1024]{1,0:T(8,128)}) custom-call(f32[8,128]{1,0:T(8,128)S(1)} %get-tuple-element.14.loss_in, bf16[512,512]{1,0:T(8,128)(2,1)S(1)} %get-tuple-element.15.gf_in, f32[6,1280,128]{2,1,0:T(8,128)S(1)} %get-tuple-element.16.gg, ...), custom_call_target="tpu_custom_call" | custom-call | tf_op jit(solution)/shard_map/finish/pallas_call | solution.py:613
